TPU v7x, 32 devices: a whole 2x2x4 slice. The times are simulated.
32 devices in a mesh: grp: 2 (over x), tp: 4 (over y, core), pp: 4 (over z).
Axes of the slice: x: 2, y: 2, z: 4, core: 2. Of those that a mesh axis runs over, the one named last changes fastest.
Arguments:
- tokens: bfloat16 [1024, 8192], P('grp', 'tp'), parts along dimension 0, may hold values from -12 to 12
- gain: bfloat16 [4, 8192], P('pp', 'tp'), may hold values from 0.099609375 to 1.8984375
- q_weight: bfloat16 [4, 8192, 4096], P('pp', None, 'tp'), may hold values from -0.5 to 0.5
- kv_weight: bfloat16 [4, 8192, 2048], P('pp', None, 'tp'), may hold values from -0.5 to 0.5
- out_weight: bfloat16 [4, 4096, 8192], P('pp', None, 'tp'), may hold values from -0.09375 to 0.09375
- page_table: int32 [4, 8, 128], P('pp'), may hold values from 0 to 1023, as said below
- segment_ids: int32 [1024], P('grp'), parts along dimension 0, may hold values from 0 to 2, never falling along the last dimension, each value on 1 to 256 neighbouring positions
Outputs:
- hidden: bfloat16 [1024, 8192], P(('grp', 'pp'), 'tp'), parts along dimension 0
- kv_cache: bfloat16 [4, 2048, 4, 256], P('pp', ('grp', 'tp')), parts along dimension 1
There are 2 independent parts, one for each index of `grp`. A program takes and returns all parts, laid end to end along the dimension named above; an argument that names none is the same for every part. Nothing has to cross between parts.
Inputs may be any that keep to these rules, and one draw needn't show every extreme that they name: `page_table`: every entry of a layer's table is distinct and every one of the 1024 values occurs once. For each layer, head and micro-batch the 16 blocks form a run; in each run half of the devices receive exactly 8 pages and the others none, so each device receives exactly 256 pages of a layer.
All inputs are finite; a program needn't handle non-finite values.
Results may differ from a plain program's by a relative error of at most 0.017.
Values may be sent and summed in bfloat16 or wider, within the bound.
A program may use at most 128 MiB of HBM per device.

v0:
```python
import math

import jax
import jax.numpy as jnp
from jax import lax
from jax.sharding import PartitionSpec as P

MODEL_WIDTH = 8192
HEAD_SIZE = 128
KEY_VALUE_HEADS = 8
PAGE_TOKENS = 4


eps_norm = 1e-05


def partner_2(x, axis, apart):
    return lax.ppermute(x, axis, [(i, i ^ 1 << apart) for i in range(lax.axis_size(axis))])


def shifted(x, axis, by):
    peers = lax.axis_size(axis)
    pairs = [(i, i + by) for i in range(peers) if 0 <= i + by < peers]
    return lax.ppermute(x, axis, pairs)


def own_pages(kv_buffer, page_rows, tp_rank, tensor_parallel_width, cache_page_count):
    row_total = kv_buffer.shape[0]
    blocks = row_total // PAGE_TOKENS
    copies = max(1, tensor_parallel_width // KEY_VALUE_HEADS)
    gathered = lax.all_gather(kv_buffer, "tp", axis=0, tiled=False)[::copies]
    head_width = 2 * HEAD_SIZE
    held = kv_buffer.shape[1] // head_width
    pages = (
        gathered.reshape(KEY_VALUE_HEADS // held, blocks, PAGE_TOKENS, held, head_width)
        .transpose(0, 3, 1, 2, 4)
        .reshape(KEY_VALUE_HEADS * blocks, PAGE_TOKENS * head_width)
    )
    slots = tp_rank * cache_page_count + jnp.arange(cache_page_count, dtype=jnp.int32)
    onehot = (page_rows.reshape(-1)[None, :] == slots[:, None]).astype(jnp.bfloat16)
    picked = jnp.dot(onehot, pages, preferred_element_type=jnp.float32).astype(jnp.bfloat16)
    return picked.reshape(cache_page_count, PAGE_TOKENS, head_width)


def body(tokens, gain, q_weight, kv_weight, out_weight, page_table, segment_ids):
    tensor_parallel_width = lax.axis_size("tp")
    pp_size = lax.axis_size("pp")
    tp_rank = lax.axis_index("tp")
    section_idx = lax.axis_index("pp")
    w_query = q_weight[0]
    w_keyval = kv_weight[0]
    w_output = out_weight[0]
    page_rows = page_table[0]
    local_width = tokens.shape[1]
    row_total = tokens.shape[0]
    micro_batches = pp_size
    row_count = row_total // micro_batches
    head_dim = HEAD_SIZE
    kv_cols = w_keyval.shape[1]
    held_heads = max(1, kv_cols // (2 * head_dim))
    q_heads = w_query.shape[1] // head_dim
    per_kv = q_heads // held_heads
    cache_page_count = KEY_VALUE_HEADS * (row_total // PAGE_TOKENS) // tensor_parallel_width
    score_scale = 1.0 / math.sqrt(head_dim)
    step_count = micro_batches + pp_size - 1
    gain_all = lax.all_gather(gain, "tp", axis=1, tiled=True).astype(jnp.float32)

    def add_columns(block_cols):
        return (
            jnp.dot(block_cols, w_query, preferred_element_type=jnp.float32),
            jnp.dot(block_cols, w_keyval, preferred_element_type=jnp.float32),
        )

    def add_outputs(block_cols):
        return jnp.dot(block_cols, w_output, preferred_element_type=jnp.float32)

    def one_step(step_idx, state_tuple):
        received, kv_buffer, hidden = state_tuple
        micro_raw = step_idx - section_idx
        is_live = (micro_raw >= 0) & (micro_raw < micro_batches)
        micro_idx = jnp.clip(micro_raw, 0, micro_batches - 1)
        row_start = micro_idx * row_count
        first_rows = lax.dynamic_slice_in_dim(tokens, row_start, row_count, 0)
        current = jnp.where(section_idx == 0, first_rows, received)
        whole_rows = lax.all_gather(current, "tp", axis=1, tiled=True).astype(jnp.float32)
        mean_sq = jnp.sum(whole_rows * whole_rows, axis=1, keepdims=True) / MODEL_WIDTH
        normed = (whole_rows * lax.rsqrt(mean_sq + eps_norm) * gain_all).astype(jnp.bfloat16)
        query_sum, keyval_sum = add_columns(normed)
        query_matrix = query_sum.astype(jnp.bfloat16)
        kv_own = keyval_sum.astype(jnp.bfloat16)
        if tensor_parallel_width > KEY_VALUE_HEADS:
            partner = partner_2(kv_own, "tp", 0)
            first_half = tp_rank % 2 == 0
            head_pair = jnp.where(
                first_half,
                jnp.concatenate([kv_own, partner], axis=1),
                jnp.concatenate([partner, kv_own], axis=1),
            )
        else:
            head_pair = kv_own
        refreshed = lax.dynamic_update_slice_in_dim(kv_buffer, head_pair, row_start, 0)
        kv_buffer = jnp.where(is_live, refreshed, kv_buffer)
        key_count = row_count * min(step_idx + 1, micro_batches)
        key_pos = jnp.arange(key_count, dtype=jnp.int32)
        kv_view = kv_buffer[:key_count].reshape(key_count, held_heads, 2, head_dim)
        grouped_queries = query_matrix.reshape(row_count, held_heads, per_kv, head_dim)
        scores = (
            jnp.einsum(
                "qgpd,kgd->gpqk",
                grouped_queries,
                kv_view[:, :, 0],
                preferred_element_type=jnp.float32,
            )
            * score_scale
        )
        query_pos = row_start + jnp.arange(row_count, dtype=jnp.int32)
        seg_query = lax.dynamic_slice_in_dim(segment_ids, row_start, row_count, 0)
        allowed = (key_pos[None, :] <= query_pos[:, None]) & (
            segment_ids[None, :key_count] == seg_query[:, None]
        )
        scores = jnp.where(allowed[None, None], scores, -1e30)
        row_max = jnp.max(scores, axis=-1, keepdims=True)
        raised = jnp.exp(scores - row_max)
        weights = (raised / jnp.sum(raised, axis=-1, keepdims=True)).astype(jnp.bfloat16)
        attended = jnp.einsum(
            "gpqk,kgd->qgpd", weights, kv_view[:, :, 1], preferred_element_type=jnp.float32
        )
        attended = attended.astype(jnp.bfloat16).reshape(row_count, q_heads * head_dim)
        projected = add_outputs(lax.all_gather(attended, "tp", axis=1, tiled=True))
        produced = (current.astype(jnp.float32) + projected).astype(jnp.bfloat16)
        done = step_idx - (pp_size - 1)
        if done >= 0:
            share = produced
            if done < pp_size - 1:
                share = lax.ppermute(produced, "pp", [(pp_size - 1, done)])
            hidden = jnp.where(section_idx == done, share, hidden)
        handed = shifted(produced, "pp", 1) if step_idx < step_count - 1 else produced
        return (handed, kv_buffer, hidden)

    initial = (
        jnp.zeros((row_count, local_width), jnp.bfloat16),
        jnp.zeros((row_total, held_heads * 2 * head_dim), jnp.bfloat16),
        jnp.zeros((row_count, local_width), jnp.bfloat16),
    )
    finished = initial
    for step_idx in range(step_count):
        finished = one_step(step_idx, finished)
    hidden = finished[2]
    kv_cache = own_pages(
        finished[1], page_rows, tp_rank, tensor_parallel_width, cache_page_count
    )
    return (hidden, kv_cache[None])


def solution(mesh):
    placed = (
        P("grp", "tp"),
        P("pp", "tp"),
        P("pp", None, "tp"),
        P("pp", None, "tp"),
        P("pp", None, "tp"),
        P("pp", None, None),
        P("grp"),
    )
    return jax.shard_map(
        body,
        mesh=mesh,
        in_specs=placed,
        out_specs=(P(("grp", "pp"), "tp"), P("pp", ("grp", "tp"), None, None)),
        check_vma=False,
    )
```

profile of v0, /device:TPU:27, one launch (start us, length us, event | category | flops | bytes accessed | tf_op | source)
XLA Modules:
  0.0 639.3 jit_solution(9808062135441615010)
XLA Ops:
  7.2 1.9 dynamic-slice_select_fusion
  9.3 5.9 all_gather.52
  17.0 17.1 %all-gather.17.cloned.1.call-done = bf16[128,8192]{1,0:T(8,128)(2,1)} async-done(((bf16[128,2048]{1,0:T(8,128)(2,1)}), bf16[128,8192]{1,0:T(8,128)(2,1)}) %all-gather.17.cloned.1.call-update) | async-done | bytes 2097168 | tf_op jit(solution)/shard_map/all_gather | solution.py:85
  34.1 2.2 fusion.49
  36.3 8.1 %fusion.90 = bf16[128,1024]{1,0:T(8,128)(2,1)S(1)} fusion(bf16[1,8192,1024]{2,1,0:T(8,128)(2,1)} %param.9, bf16[128,8192]{1,0:T(8,128)(2,1)S(1)} %copy-done.9, f32[8192]{0:T(1024)S(1)} %bitcast.384, f32[128]{0:T(128)S(1)} %add_rsqrt_fusion.6), kind=kOutput, calls=%fused_computation.124 | convolution fusion | flops 2151809024 | bytes 19169792 | tf_op jit(solution)/shard_map/dot_general | solution.py:70
  44.7 4.7 fusion.171
  51.3 16.8 %all-gather.19.cloned.1.call-done = bf16[128,4096]{0,1:T(8,128)(2,1)} async-done(((bf16[128,1024]{0,1:T(8,128)(2,1)}), bf16[128,4096]{0,1:T(8,128)(2,1)}) %all-gather.19.cloned.1.call-update) | async-done | bytes 1048592 | tf_op jit(solution)/shard_map/all_gather | solution.py:129
  68.1 8.5 %fusion.73 = bf16[128,2048]{1,0:T(8,128)(2,1)S(1)} fusion(bf16[128,4096]{0,1:T(8,128)(2,1)} %all-gather.19.cloned.1.call-done, bf16[1,4096,2048]{2,1,0:T(8,128)(2,1)} %param.11, bf16[128,2048]{1,0:T(8,128)(2,1)S(1)} %copy-done.2), kind=kOutput, calls=%fused_computation.85 | convolution fusion | flops 2148270080 | bytes 18874368 | tf_op jit(solution)/shard_map/dot_general | solution.py:75
  77.8 13.8 %collective-permute-done = bf16[128,2048]{1,0:T(8,128)(2,1)S(1)} collective-permute-done((bf16[128,2048]{1,0:T(8,128)(2,1)S(1)}, bf16[128,2048]{1,0:T(8,128)(2,1)S(1)}, u32[]{:S(2)}, u32[]{:S(2)}) %collective-permute-start) | collective-permute-done | bytes 524320 | tf_op jit(solution)/shard_map/ppermute | solution.py:24
  93.0 23.2 %all-gather.21.cloned.1.call-done = bf16[128,8192]{1,0:T(8,128)(2,1)} async-done(((bf16[128,2048]{1,0:T(8,128)(2,1)}), bf16[128,8192]{1,0:T(8,128)(2,1)}) %all-gather.21.cloned.1.call-update) | async-done | bytes 2097168 | tf_op jit(solution)/shard_map/all_gather | solution.py:85
  116.2 2.2 fusion.52
  118.4 8.3 %fusion.93 = bf16[128,1024]{1,0:T(8,128)(2,1)S(1)} fusion(bf16[1,8192,1024]{2,1,0:T(8,128)(2,1)} %param.9, bf16[128,8192]{1,0:T(8,128)(2,1)S(1)} %copy-done.11, f32[128]{0:T(128)S(1)} %add_rsqrt_fusion.5, f32[8192]{0:T(1024)S(1)} %bitcast.386), kind=kOutput, calls=%fused_computation.125 | convolution fusion | flops 2151809024 | bytes 19169792 | tf_op jit(solution)/shard_map/dot_general | solution.py:70
  126.9 5.3 fusion.165
  136.3 2.7 convolution_convert_fusion.5
  139.1 16.8 %all-gather.23.cloned.1.call-done = bf16[128,4096]{0,1:T(8,128)(2,1)} async-done(((bf16[128,1024]{0,1:T(8,128)(2,1)}), bf16[128,4096]{0,1:T(8,128)(2,1)}) %all-gather.23.cloned.1.call-update) | async-done | bytes 1048592 | tf_op jit(solution)/shard_map/all_gather | solution.py:129
  155.9 8.5 %add_convert_fusion.5 = bf16[128,2048]{1,0:T(8,128)(2,1)S(1)} fusion(bf16[128,2048]{1,0:T(8,128)(2,1)S(1)} %copy-done.5, bf16[128,4096]{0,1:T(8,128)(2,1)} %all-gather.23.cloned.1.call-done, bf16[1,4096,2048]{2,1,0:T(8,128)(2,1)} %param.11), kind=kOutput, calls=%fused_computation.165 | convolution fusion | flops 2148270080 | bytes 18874368 | tf_op jit(solution)/shard_map/dot_general | solution.py:75
  165.7 13.8 %collective-permute-done.1 = bf16[128,2048]{1,0:T(8,128)(2,1)S(1)} collective-permute-done((bf16[128,2048]{1,0:T(8,128)(2,1)S(1)}, bf16[128,2048]{1,0:T(8,128)(2,1)S(1)}, u32[]{:S(2)}, u32[]{:S(2)}) %collective-permute-start.1) | collective-permute-done | bytes 524320 | tf_op jit(solution)/shard_map/ppermute | solution.py:24
  180.9 23.1 %all-gather.25.cloned.1.call-done = bf16[128,8192]{1,0:T(8,128)(2,1)} async-done(((bf16[128,2048]{1,0:T(8,128)(2,1)}), bf16[128,8192]{1,0:T(8,128)(2,1)}) %all-gather.25.cloned.1.call-update) | async-done | bytes 2097168 | tf_op jit(solution)/shard_map/all_gather | solution.py:85
  204.0 2.2 fusion.55
  206.3 8.3 %fusion.96 = bf16[128,1024]{1,0:T(8,128)(2,1)S(1)} fusion(bf16[1,8192,1024]{2,1,0:T(8,128)(2,1)} %param.9, bf16[128,8192]{1,0:T(8,128)(2,1)S(1)} %copy-done.12, f32[128]{0:T(128)S(1)} %add_rsqrt_fusion.4, f32[8192]{0:T(1024)S(1)} %bitcast.388), kind=kOutput, calls=%fused_computation.126 | convolution fusion | flops 2151809024 | bytes 19169792 | tf_op jit(solution)/shard_map/dot_general | solution.py:70
  215.4 5.3 fusion.159
  223.3 2.9 fusion.326
  226.3 2.5 convolution_convert_fusion.7
  228.8 16.8 %all-gather.27.cloned.1.call-done = bf16[128,4096]{0,1:T(8,128)(2,1)} async-done(((bf16[128,1024]{0,1:T(8,128)(2,1)}), bf16[128,4096]{0,1:T(8,128)(2,1)}) %all-gather.27.cloned.1.call-update) | async-done | bytes 1048592 | tf_op jit(solution)/shard_map/all_gather | solution.py:129
  245.6 8.5 %add_convert_fusion.4 = bf16[128,2048]{1,0:T(8,128)(2,1)S(1)} fusion(bf16[128,2048]{1,0:T(8,128)(2,1)S(1)} %copy-done.6, bf16[128,4096]{0,1:T(8,128)(2,1)} %all-gather.27.cloned.1.call-done, bf16[1,4096,2048]{2,1,0:T(8,128)(2,1)} %param.11), kind=kOutput, calls=%fused_computation.164 | convolution fusion | flops 2148270080 | bytes 18874368 | tf_op jit(solution)/shard_map/dot_general | solution.py:75
  255.4 13.8 %collective-permute-done.2 = bf16[128,2048]{1,0:T(8,128)(2,1)S(1)} collective-permute-done((bf16[128,2048]{1,0:T(8,128)(2,1)S(1)}, bf16[128,2048]{1,0:T(8,128)(2,1)S(1)}, u32[]{:S(2)}, u32[]{:S(2)}) %collective-permute-start.2) | collective-permute-done | bytes 524320 | tf_op jit(solution)/shard_map/ppermute | solution.py:24
  271.6 22.1 %all-gather.29.cloned.1.call-done = bf16[128,8192]{1,0:T(8,128)(2,1)} async-done(((bf16[128,2048]{1,0:T(8,128)(2,1)}), bf16[128,8192]{1,0:T(8,128)(2,1)}) %all-gather.29.cloned.1.call-update) | async-done | bytes 2097168 | tf_op jit(solution)/shard_map/all_gather | solution.py:85
  293.7 2.2 fusion.58
  296.0 8.3 %fusion.99 = bf16[128,1024]{1,0:T(8,128)(2,1)S(1)} fusion(bf16[1,8192,1024]{2,1,0:T(8,128)(2,1)} %param.9, bf16[128,8192]{1,0:T(8,128)(2,1)S(1)} %copy-done.10, f32[128]{0:T(128)S(1)} %add_rsqrt_fusion.3, f32[8192]{0:T(1024)S(1)} %bitcast.390), kind=kOutput, calls=%fused_computation.127 | convolution fusion | flops 2151809024 | bytes 19169792 | tf_op jit(solution)/shard_map/dot_general | solution.py:70
  305.1 5.3 fusion.153
  313.5 2.0 fusion.329
  315.5 3.0 convolution_convert_fusion.4
  318.6 16.8 %all-gather.31.cloned.1.call-done = bf16[128,4096]{0,1:T(8,128)(2,1)} async-done(((bf16[128,1024]{0,1:T(8,128)(2,1)}), bf16[128,4096]{0,1:T(8,128)(2,1)}) %all-gather.31.cloned.1.call-update) | async-done | bytes 1048592 | tf_op jit(solution)/shard_map/all_gather | solution.py:129
  335.4 8.5 %add_convert_fusion.3 = bf16[128,2048]{1,0:T(8,128)(2,1)S(1)} fusion(bf16[128,2048]{1,0:T(8,128)(2,1)S(1)} %copy-done.4, bf16[128,4096]{0,1:T(8,128)(2,1)} %all-gather.31.cloned.1.call-done, bf16[1,4096,2048]{2,1,0:T(8,128)(2,1)} %param.11), kind=kOutput, calls=%fused_computation.155 | convolution fusion | flops 2148270080 | bytes 18874368 | tf_op jit(solution)/shard_map/dot_general | solution.py:75
  346.1 13.8 %collective-permute-done.3 = bf16[128,2048]{1,0:T(8,128)(2,1)S(1)} collective-permute-done((bf16[128,2048]{1,0:T(8,128)(2,1)S(1)}, bf16[128,2048]{1,0:T(8,128)(2,1)S(1)}, u32[]{:S(2)}, u32[]{:S(2)}) %collective-permute-start.3) | collective-permute-done | bytes 524320 | tf_op jit(solution)/shard_map/ppermute | solution.py:24
  361.1 23.3 %all-gather.33.cloned.1.call-done = bf16[128,8192]{1,0:T(8,128)(2,1)} async-done(((bf16[128,2048]{1,0:T(8,128)(2,1)}), bf16[128,8192]{1,0:T(8,128)(2,1)}) %all-gather.33.cloned.1.call-update) | async-done | bytes 2097168 | tf_op jit(solution)/shard_map/all_gather | solution.py:85
  384.4 2.2 fusion.61
  386.7 8.3 %fusion.102 = bf16[128,1024]{1,0:T(8,128)(2,1)S(1)} fusion(bf16[1,8192,1024]{2,1,0:T(8,128)(2,1)} %param.9, bf16[128,8192]{1,0:T(8,128)(2,1)S(1)} %copy-done.14, f32[128]{0:T(128)S(1)} %add_rsqrt_fusion.2, f32[8192]{0:T(1024)S(1)} %bitcast.392), kind=kOutput, calls=%fused_computation.128 | convolution fusion | flops 2151809024 | bytes 19169792 | tf_op jit(solution)/shard_map/dot_general | solution.py:70
  395.8 5.3 fusion.147
  404.2 2.0 fusion.332
  406.2 3.0 convolution_convert_fusion.3
  409.3 16.8 %all-gather.35.cloned.1.call-done = bf16[128,4096]{0,1:T(8,128)(2,1)} async-done(((bf16[128,1024]{0,1:T(8,128)(2,1)}), bf16[128,4096]{0,1:T(8,128)(2,1)}) %all-gather.35.cloned.1.call-update) | async-done | bytes 1048592 | tf_op jit(solution)/shard_map/all_gather | solution.py:129
  426.1 8.5 %add_convert_fusion.2 = bf16[128,2048]{1,0:T(8,128)(2,1)S(1)} fusion(bf16[128,2048]{1,0:T(8,128)(2,1)S(1)} %copy-done.7, bf16[128,4096]{0,1:T(8,128)(2,1)} %all-gather.35.cloned.1.call-done, bf16[1,4096,2048]{2,1,0:T(8,128)(2,1)} %param.11), kind=kOutput, calls=%fused_computation.154 | convolution fusion | flops 2148270080 | bytes 18874368 | tf_op jit(solution)/shard_map/dot_general | solution.py:75
  436.8 13.8 %collective-permute-done.4 = bf16[128,2048]{1,0:T(8,128)(2,1)S(1)} collective-permute-done((bf16[128,2048]{1,0:T(8,128)(2,1)S(1)}, bf16[128,2048]{1,0:T(8,128)(2,1)S(1)}, u32[]{:S(2)}, u32[]{:S(2)}) %collective-permute-start.4) | collective-permute-done | bytes 524320 | tf_op jit(solution)/shard_map/ppermute | solution.py:24
  451.8 23.3 %all-gather.37.cloned.1.call-done = bf16[128,8192]{1,0:T(8,128)(2,1)} async-done(((bf16[128,2048]{1,0:T(8,128)(2,1)}), bf16[128,8192]{1,0:T(8,128)(2,1)}) %all-gather.37.cloned.1.call-update) | async-done | bytes 2097168 | tf_op jit(solution)/shard_map/all_gather | solution.py:85
  475.1 2.2 fusion.64
  477.4 8.3 %fusion.105 = bf16[128,1024]{1,0:T(8,128)(2,1)S(1)} fusion(bf16[1,8192,1024]{2,1,0:T(8,128)(2,1)} %param.9, bf16[128,8192]{1,0:T(8,128)(2,1)S(1)} %copy-done.15, f32[128]{0:T(128)S(1)} %add_rsqrt_fusion.1, f32[8192]{0:T(1024)S(1)} %bitcast.394), kind=kOutput, calls=%fused_computation.129 | convolution fusion | flops 2151809024 | bytes 19169792 | tf_op jit(solution)/shard_map/dot_general | solution.py:70
  486.5 5.3 fusion.141
  494.9 2.0 fusion.335
  496.9 3.0 convolution_convert_fusion.2
  500.0 16.8 %all-gather.39.cloned.1.call-done = bf16[128,4096]{0,1:T(8,128)(2,1)} async-done(((bf16[128,1024]{0,1:T(8,128)(2,1)}), bf16[128,4096]{0,1:T(8,128)(2,1)}) %all-gather.39.cloned.1.call-update) | async-done | bytes 1048592 | tf_op jit(solution)/shard_map/all_gather | solution.py:129
  516.8 8.5 %add_convert_fusion.1 = bf16[128,2048]{1,0:T(8,128)(2,1)S(1)} fusion(bf16[128,2048]{1,0:T(8,128)(2,1)S(1)} %copy-done.8, bf16[128,4096]{0,1:T(8,128)(2,1)} %all-gather.39.cloned.1.call-done, bf16[1,4096,2048]{2,1,0:T(8,128)(2,1)} %param.11), kind=kOutput, calls=%fused_computation.153 | convolution fusion | flops 2148270080 | bytes 18874368 | tf_op jit(solution)/shard_map/dot_general | solution.py:75
  527.4 13.8 %collective-permute-done.5 = bf16[128,2048]{1,0:T(8,128)(2,1)S(1)} collective-permute-done((bf16[128,2048]{1,0:T(8,128)(2,1)S(1)}, bf16[128,2048]{1,0:T(8,128)(2,1)S(1)}, u32[]{:S(2)}, u32[]{:S(2)}) %collective-permute-start.5) | collective-permute-done | bytes 524320 | tf_op jit(solution)/shard_map/ppermute | solution.py:24
  542.5 23.3 %all-gather.41.cloned.1.call-done = bf16[128,8192]{1,0:T(8,128)(2,1)} async-done(((bf16[128,2048]{1,0:T(8,128)(2,1)}), bf16[128,8192]{1,0:T(8,128)(2,1)}) %all-gather.41.cloned.1.call-update) | async-done | bytes 2097168 | tf_op jit(solution)/shard_map/all_gather | solution.py:85
  565.8 2.2 fusion.67
  568.0 8.2 %fusion.108 = bf16[128,1024]{1,0:T(8,128)(2,1)S(1)} fusion(bf16[1,8192,1024]{2,1,0:T(8,128)(2,1)} %param.9, bf16[128,8192]{1,0:T(8,128)(2,1)S(1)} %copy-done.13, f32[128]{0:T(128)S(1)} %add_rsqrt_fusion, f32[8192]{0:T(1024)S(1)} %bitcast.396), kind=kOutput, calls=%fused_computation.130 | convolution fusion | flops 2151809024 | bytes 19169792 | tf_op jit(solution)/shard_map/dot_general | solution.py:70
  576.4 4.7 fusion.135
  586.0 2.3 collective-permute-start.8
  589.6 2.4 collective-permute-start.6
  592.0 10.2 %all-gather.43.cloned.1.call-done = bf16[128,4096]{0,1:T(8,128)(2,1)} async-done(((bf16[128,1024]{0,1:T(8,128)(2,1)}), bf16[128,4096]{0,1:T(8,128)(2,1)}) %all-gather.43.cloned.1.call-update) | async-done | bytes 1048592 | tf_op jit(solution)/shard_map/all_gather | solution.py:129
  602.2 8.5 %fusion.7 = f32[128,2048]{1,0:T(8,128)S(1)} fusion(bf16[128,4096]{0,1:T(8,128)(2,1)} %all-gather.43.cloned.1.call-done, bf16[1,4096,2048]{2,1,0:T(8,128)(2,1)} %param.11), kind=kOutput, calls=%fused_computation.7 | convolution fusion | flops 2147483648 | bytes 18874368 | tf_op jit(solution)/shard_map/dot_general | solution.py:75
  610.7 11.0 %collective-permute-done.6 = bf16[128,2048]{1,0:T(8,128)(2,1)} collective-permute-done((bf16[128,2048]{1,0:T(8,128)(2,1)S(1)}, bf16[128,2048]{1,0:T(8,128)(2,1)}, u32[]{:S(2)}, u32[]{:S(2)}) %collective-permute-start.6) | collective-permute-done | bytes 524320 | tf_op jit(solution)/shard_map/ppermute | solution.py:135
  622.7 3.5 all-gather.45.cloned.1.call-done
  626.2 2.5 reshape.520
  (171 shorter events, 53.8 us)
Async XLA Ops:
  7.2 26.9 %all-gather.17.cloned.1.call-start = ((), (), s32[]{:S(2)}) async-start(), calls=%async_computation | async-start | bytes 2621440 | tf_op jit(solution)/shard_map/all_gather | solution.py:85
  9.2 58.9 %all-gather.19.cloned.1.call-start = ((), (), s32[]{:S(2)}) async-start(), calls=%async_computation.1 | async-start | bytes 1310720 | tf_op jit(solution)/shard_map/all_gather | solution.py:129
  15.2 200.2 %copy-start.25 = (f32[1,8192]{1,0:T(1,128)}, f32[1,8192]{1,0:T(1,128)S(1)}, u32[]{:S(2)}) copy-start(f32[1,8192]{1,0:T(1,128)S(1)} %mul.257) | copy-start | bytes 98308
  34.1 2.2 copy-start.9
  49.5 18.5 %copy-start.2 = (bf16[128,2048]{1,0:T(8,128)(2,1)S(1)}, bf16[128,2048]{1,0:T(8,128)(2,1)}, u32[]{:S(2)}) copy-start(bf16[128,2048]{1,0:T(8,128)(2,1)} %dynamic-slice_select_fusion) | copy-start | bytes 1572868
  51.2 40.4 %copy-start.1 = (bf16[512,2048]{1,0:T(8,128)(2,1)S(1)}, bf16[512,2048]{1,0:T(8,128)(2,1)}, u32[]{:S(2)}) copy-start(bf16[512,2048]{1,0:T(8,128)(2,1)} %param.7) | copy-start | bytes 6291460
  51.2 64.9 %all-gather.21.cloned.1.call-start = ((), (), s32[]{:S(2)}) async-start(), calls=%async_computation.2 | async-start | bytes 2621440 | tf_op jit(solution)/shard_map/all_gather | solution.py:85
  76.5 16.3 %slice-start = ((s32[512]{0:T(512)}), s32[256]{0:T(256)S(1)}, s32[]{:S(2)}) async-start(s32[512]{0:T(512)} %param.13), calls=%async_computation.15 | async-start | bytes 2048 | tf_op jit(solution)/shard_map/slice | solution.py:119
  76.5 15.1 %collective-permute-start = (bf16[128,2048]{1,0:T(8,128)(2,1)S(1)}, bf16[128,2048]{1,0:T(8,128)(2,1)S(1)}, u32[]{:S(2)}, u32[]{:S(2)}) collective-permute-start(bf16[128,2048]{1,0:T(8,128)(2,1)S(1)} %fusion.73), channel_id=1, source_target_pairs={{0,1},{1,2},{2,3},{4,5},{5,6},{6,7},{8,9},{9,10},{10,11},{12,13},{... | collective-permute-start | bytes 1572872 | tf_op jit(solution)/shard_map/ppermute | solution.py:24
  92.6 63.3 %all-gather.23.cloned.1.call-start = ((), (), s32[]{:S(2)}) async-start(), calls=%async_computation.3 | async-start | bytes 1310720 | tf_op jit(solution)/shard_map/all_gather | solution.py:129
  116.2 2.2 copy-start.11
  133.4 1.5 copy-start.16
  136.3 19.6 %copy-start.5 = (bf16[128,2048]{1,0:T(8,128)(2,1)S(1)}, bf16[128,2048]{1,0:T(8,128)(2,1)}, u32[]{:S(2)}) copy-start(bf16[128,2048]{1,0:T(8,128)(2,1)} %dynamic-slice_select_fusion.1) | copy-start | bytes 1572868
  139.1 64.9 %all-gather.25.cloned.1.call-start = ((), (), s32[]{:S(2)}) async-start(), calls=%async_computation.4 | async-start | bytes 2621440 | tf_op jit(solution)/shard_map/all_gather | solution.py:85
  164.4 16.4 %copy-start.24 = (s32[512]{0:T(512)S(1)}, s32[512]{0:T(512)}, u32[]{:S(2)}) copy-start(s32[512]{0:T(512)} %param.13) | copy-start | bytes 6148
  164.4 15.1 %collective-permute-start.1 = (bf16[128,2048]{1,0:T(8,128)(2,1)S(1)}, bf16[128,2048]{1,0:T(8,128)(2,1)S(1)}, u32[]{:S(2)}, u32[]{:S(2)}) collective-permute-start(bf16[128,2048]{1,0:T(8,128)(2,1)S(1)} %add_convert_fusion.5), channel_id=1, source_target_pairs={{0,1},{1,2},{2,3},{4,5},{5,6},{6,7},{8,9},{9,10},{10,11},{12,13},{... | collective-permute-start | bytes 1572872 | tf_op jit(solution)/shard_map/ppermute | solution.py:24
  180.4 65.2 %all-gather.27.cloned.1.call-start = ((), (), s32[]{:S(2)}) async-start(), calls=%async_computation.5 | async-start | bytes 1310720 | tf_op jit(solution)/shard_map/all_gather | solution.py:129
  204.0 2.2 copy-start.12
  223.3 2.9 copy-start.23
  226.3 19.3 %copy-start.6 = (bf16[128,2048]{1,0:T(8,128)(2,1)S(1)}, bf16[128,2048]{1,0:T(8,128)(2,1)}, u32[]{:S(2)}) copy-start(bf16[128,2048]{1,0:T(8,128)(2,1)} %dynamic-slice_select_fusion.2) | copy-start | bytes 1572868
  228.8 64.9 %all-gather.29.cloned.1.call-start = ((), (), s32[]{:S(2)}) async-start(), calls=%async_computation.6 | async-start | bytes 2621440 | tf_op jit(solution)/shard_map/all_gather | solution.py:85
  254.1 16.6 %copy-start.30 = (s32[128]{0:T(128)S(1)}, s32[128]{0:T(128)}, u32[]{:S(2)}) copy-start(s32[128]{0:T(128)} %get-tuple-element.25) | copy-start | bytes 1540
  254.1 41.9 %copy-start.26 = (f32[1,8192]{1,0:T(1,128)S(1)}, f32[1,8192]{1,0:T(1,128)}, u32[]{:S(2)}) copy-start(f32[1,8192]{1,0:T(1,128)} %copy-done.25) | copy-start | bytes 98308
  254.1 15.1 %collective-permute-start.2 = (bf16[128,2048]{1,0:T(8,128)(2,1)S(1)}, bf16[128,2048]{1,0:T(8,128)(2,1)S(1)}, u32[]{:S(2)}, u32[]{:S(2)}) collective-permute-start(bf16[128,2048]{1,0:T(8,128)(2,1)S(1)} %add_convert_fusion.4), channel_id=1, source_target_pairs={{0,1},{1,2},{2,3},{4,5},{5,6},{6,7},{8,9},{9,10},{10,11},{12,13},{... | collective-permute-start | bytes 1572872 | tf_op jit(solution)/shard_map/ppermute | solution.py:24
  270.1 65.3 %all-gather.31.cloned.1.call-start = ((), (), s32[]{:S(2)}) async-start(), calls=%async_computation.7 | async-start | bytes 1310720 | tf_op jit(solution)/shard_map/all_gather | solution.py:129
  293.7 2.3 copy-start.10
  315.5 19.9 %copy-start.4 = (bf16[128,2048]{1,0:T(8,128)(2,1)S(1)}, bf16[128,2048]{1,0:T(8,128)(2,1)}, u32[]{:S(2)}) copy-start(bf16[128,2048]{1,0:T(8,128)(2,1)} %dynamic-slice_select_fusion.3) | copy-start | bytes 1572868
  318.5 65.9 %all-gather.33.cloned.1.call-start = ((), (), s32[]{:S(2)}) async-start(), calls=%async_computation.8 | async-start | bytes 2621440 | tf_op jit(solution)/shard_map/all_gather | solution.py:85
  343.9 0.8 copy-start.17
  344.7 42.0 %copy-start.27 = (f32[1,8192]{1,0:T(1,128)S(1)}, f32[1,8192]{1,0:T(1,128)}, u32[]{:S(2)}) copy-start(f32[1,8192]{1,0:T(1,128)} %copy-done.25) | copy-start | bytes 98308
  344.7 15.2 %collective-permute-start.3 = (bf16[128,2048]{1,0:T(8,128)(2,1)S(1)}, bf16[128,2048]{1,0:T(8,128)(2,1)S(1)}, u32[]{:S(2)}, u32[]{:S(2)}) collective-permute-start(bf16[128,2048]{1,0:T(8,128)(2,1)S(1)} %add_convert_fusion.3), channel_id=1, source_target_pairs={{0,1},{1,2},{2,3},{4,5},{5,6},{6,7},{8,9},{9,10},{10,11},{12,13},{... | collective-permute-start | bytes 1572872 | tf_op jit(solution)/shard_map/ppermute | solution.py:24
  360.8 65.3 %all-gather.35.cloned.1.call-start = ((), (), s32[]{:S(2)}) async-start(), calls=%async_computation.9 | async-start | bytes 1310720 | tf_op jit(solution)/shard_map/all_gather | solution.py:129
  384.4 2.3 copy-start.14
  406.2 19.9 %copy-start.7 = (bf16[128,2048]{1,0:T(8,128)(2,1)S(1)}, bf16[128,2048]{1,0:T(8,128)(2,1)}, u32[]{:S(2)}) copy-start(bf16[128,2048]{1,0:T(8,128)(2,1)} %dynamic-slice_select_fusion.4) | copy-start | bytes 1572868
  409.3 65.9 %all-gather.37.cloned.1.call-start = ((), (), s32[]{:S(2)}) async-start(), calls=%async_computation.10 | async-start | bytes 2621440 | tf_op jit(solution)/shard_map/all_gather | solution.py:85
  434.6 0.8 copy-start.19
  435.4 42.0 %copy-start.28 = (f32[1,8192]{1,0:T(1,128)S(1)}, f32[1,8192]{1,0:T(1,128)}, u32[]{:S(2)}) copy-start(f32[1,8192]{1,0:T(1,128)} %copy-done.25) | copy-start | bytes 98308
  435.4 15.2 %collective-permute-start.4 = (bf16[128,2048]{1,0:T(8,128)(2,1)S(1)}, bf16[128,2048]{1,0:T(8,128)(2,1)S(1)}, u32[]{:S(2)}, u32[]{:S(2)}) collective-permute-start(bf16[128,2048]{1,0:T(8,128)(2,1)S(1)} %add_convert_fusion.2), channel_id=1, source_target_pairs={{0,1},{1,2},{2,3},{4,5},{5,6},{6,7},{8,9},{9,10},{10,11},{12,13},{... | collective-permute-start | bytes 1572872 | tf_op jit(solution)/shard_map/ppermute | solution.py:24
  451.5 65.2 %all-gather.39.cloned.1.call-start = ((), (), s32[]{:S(2)}) async-start(), calls=%async_computation.11 | async-start | bytes 1310720 | tf_op jit(solution)/shard_map/all_gather | solution.py:129
  475.1 2.3 copy-start.15
  496.9 19.8 %copy-start.8 = (bf16[128,2048]{1,0:T(8,128)(2,1)S(1)}, bf16[128,2048]{1,0:T(8,128)(2,1)}, u32[]{:S(2)}) copy-start(bf16[128,2048]{1,0:T(8,128)(2,1)} %dynamic-slice_select_fusion.5) | copy-start | bytes 1572868
  499.9 65.8 %all-gather.41.cloned.1.call-start = ((), (), s32[]{:S(2)}) async-start(), calls=%async_computation.12 | async-start | bytes 2621440 | tf_op jit(solution)/shard_map/all_gather | solution.py:85
  525.2 0.8 copy-start.21
  526.0 42.0 %copy-start.29 = (f32[1,8192]{1,0:T(1,128)S(1)}, f32[1,8192]{1,0:T(1,128)}, u32[]{:S(2)}) copy-start(f32[1,8192]{1,0:T(1,128)} %copy-done.25) | copy-start | bytes 98308
  526.0 15.2 %collective-permute-start.5 = (bf16[128,2048]{1,0:T(8,128)(2,1)S(1)}, bf16[128,2048]{1,0:T(8,128)(2,1)S(1)}, u32[]{:S(2)}, u32[]{:S(2)}) collective-permute-start(bf16[128,2048]{1,0:T(8,128)(2,1)S(1)} %add_convert_fusion.1), channel_id=1, source_target_pairs={{0,1},{1,2},{2,3},{4,5},{5,6},{6,7},{8,9},{9,10},{10,11},{12,13},{... | collective-permute-start | bytes 1572872 | tf_op jit(solution)/shard_map/ppermute | solution.py:24
  542.2 60.0 %all-gather.43.cloned.1.call-start = ((), (), s32[]{:S(2)}) async-start(), calls=%async_computation.13 | async-start | bytes 1310720 | tf_op jit(solution)/shard_map/all_gather | solution.py:129
  565.8 2.3 copy-start.13
  581.0 2.4 copy-start
  583.5 2.5 copy-start.18
  583.5 4.8 copy-start.20
  583.5 6.1 copy-start.22
  585.4 40.9 %all-gather.45.cloned.1.call-start = ((), (), s32[]{:S(2)}) async-start(), calls=%async_computation.14 | async-start | bytes 2621440 | tf_op jit(solution)/shard_map/all_gather | solution.py:31
  586.0 35.7 %copy-start.3 = (bf16[128,2048]{1,0:T(8,128)(2,1)S(1)}, bf16[128,2048]{1,0:T(8,128)(2,1)}, u32[]{:S(2)}) copy-start(bf16[128,2048]{1,0:T(8,128)(2,1)} %dynamic-slice_select_fusion.6) | copy-start | bytes 1572868
  586.0 24.7 %collective-permute-start.8 = (bf16[128,2048]{1,0:T(8,128)(2,1)S(1)}, bf16[128,2048]{1,0:T(8,128)(2,1)S(1)}, u32[]{:S(2)}, u32[]{:S(2)}) collective-permute-start(bf16[128,2048]{1,0:T(8,128)(2,1)S(1)} %copy-done.18), channel_id=1, source_target_pairs={{3,0},{7,4},{11,8},{15,12},{19,16},{23,20},{27,24},{31,28}} | collective-permute-start | bytes 1572872 | tf_op jit(solution)/shard_map/ppermute | solution.py:135
  588.3 22.4 %collective-permute-start.7 = (bf16[128,2048]{1,0:T(8,128)(2,1)S(1)}, bf16[128,2048]{1,0:T(8,128)(2,1)S(1)}, u32[]{:S(2)}, u32[]{:S(2)}) collective-permute-start(bf16[128,2048]{1,0:T(8,128)(2,1)S(1)} %copy-done.20), channel_id=1, source_target_pairs={{3,1},{7,5},{11,9},{15,13},{19,17},{23,21},{27,25},{31,29}} | collective-permute-start | bytes 1572872 | tf_op jit(solution)/shard_map/ppermute | solution.py:135
  589.6 32.1 %collective-permute-start.6 = (bf16[128,2048]{1,0:T(8,128)(2,1)S(1)}, bf16[128,2048]{1,0:T(8,128)(2,1)}, u32[]{:S(2)}, u32[]{:S(2)}) collective-permute-start(bf16[128,2048]{1,0:T(8,128)(2,1)S(1)} %copy-done.22), channel_id=1, source_target_pairs={{3,2},{7,6},{11,10},{15,14},{19,18},{23,22},{27,26},{31,30}} | collective-permute-start | bytes 1572872 | tf_op jit(solution)/shard_map/ppermute | solution.py:135
  629.6 0.7 copy-start.31
Sparse Core Ops, SparseCore 0:
  10.1 23.9 all-gather.16
  51.3 16.6 all-gather.18
  92.7 23.4 all-gather.20
  139.2 16.6 all-gather.22
  180.5 23.4 all-gather.24
  228.9 16.6 all-gather.26
  270.2 23.4 all-gather.28
  318.7 16.6 all-gather.30
  361.0 23.4 all-gather.32
  409.4 16.6 all-gather.34
  451.7 23.4 all-gather.36
  500.0 16.6 all-gather.38
  542.3 23.4 all-gather.40
  585.5 16.6 all-gather.42
  603.6 22.5 all-gather.44
where the time goes:
time: 648 us; the launch traced here: 639 us
  waiting for transfers between devices  364 us (56%)
  matrix products  184 us (28%)
  other arithmetic  27.1 us (4%)
  local copies, waits for them, and re-layouts  26.5 us (4%)
  starting transfers between devices  16.3 us (3%)
  between operations  15.4 us (2%)
    all_gather x7, waiting for transfers between devices, one_step(): lax.all_gather(current, 'tp', axis=1, tiled=True).astype(jnp.float32)  155 us
    all_gather x7, waiting for transfers between devices, one_step(): projected = add_outputs(lax.all_gather(attended, 'tp', axis=1, tiled=True))  111 us
    ppermute x6, waiting for transfers between devices, shifted(): return lax.ppermute(x, axis, pairs)  82.7 us
    dot_general x7, matrix products, add_outputs(): return jnp.dot(block_cols, w_output, preferred_element_type=jnp.float32)  59.3 us
    dot_general x7, matrix products, add_columns(): jnp.dot(block_cols, w_query, preferred_element_type=jnp.float32)  57.6 us
    dot_general x7, matrix products, add_columns(): jnp.dot(block_cols, w_keyval, preferred_element_type=jnp.float32)  36 us
    dot_general x7, matrix products, one_step(): jnp.einsum('gpqk,kgd->qgpd', weights, kv_view[:, :, 1], preferred_element...  17 us
    reduce_sum x7, other arithmetic, one_step(): jnp.sum(whole_rows * whole_rows, axis=1, keepdims=True) / MODEL_WIDTH  15.6 us
  transfers between devices with their start and end apart: 24, of which 22 were waited for; matrix products, arithmetic and copies ran while one was open for 2% of the time, Pallas kernels for 0%

commit v1 on v0

--- a/solution.py
+++ b/solution.py
@@ -1,8 +1,11 @@
+import functools
 import math
 
 import jax
 import jax.numpy as jnp
 from jax import lax
+from jax.experimental import pallas as pl
+from jax.experimental.pallas import tpu as pltpu
 from jax.sharding import PartitionSpec as P
 
 MODEL_WIDTH = 8192
@@ -152,6 +155,471 @@
     return (hidden, kv_cache[None])
 
 
+MESH = pl.DeviceIdType.MESH
+LANES = 128
+STREAM_CHUNKS = 2
+
+
+def section_kernel(
+    rows_of_mb,
+    micro_batches,
+    pp_size,
+    tokens_hbm,
+    gain_ref,
+    wq_hbm,
+    wkv_hbm,
+    wo_hbm,
+    ids_ref,
+    seg_row_ref,
+    seg_col_ref,
+    hidden_hbm,
+    cache_hbm,
+    wq,
+    wkv,
+    wo,
+    stream,
+    attended,
+    keyval,
+    gains,
+    scaled,
+    acc,
+    proj,
+    squares,
+    landed,
+    cache,
+    wq_sem,
+    wkv_sem,
+    wo_sem,
+    token_sem,
+    gain_send,
+    gain_recv,
+    z_send,
+    z_recv,
+    y_send,
+    y_recv,
+    d_send,
+    d_recv,
+    r_send,
+    r_recv,
+    ay_send,
+    ay_recv,
+    ad_send,
+    ad_recv,
+    ar_send,
+    ar_recv,
+    k_send,
+    k_recv,
+    h_send,
+    h_recv,
+    out_sem,
+):
+    R, M, C = rows_of_mb, micro_batches, STREAM_CHUNKS
+    width = stream.shape[2]
+    model_width = 4 * width
+    att_width = attended.shape[2]
+    kv_width = keyval.shape[2]
+    total_rows = stream.shape[1]
+    q_width = wq.shape[1]
+    chunk = width // C
+    t = lax.axis_index("tp")
+    sec = lax.axis_index("pp")
+    last = pp_size - 1
+    core = t % 2
+    near = t + 1 - 2 * core
+    far = (t + 2) % 4
+    cross = (near + 2) % 4
+    sources = (t, near, far, cross)
+    score_scale = 1.0 / math.sqrt(HEAD_SIZE)
+    per_section = M // pp_size
+
+    def rows(i):
+        return pl.ds(pl.multiple_of(i * R, R), R)
+
+    def cols(c):
+        return pl.ds(c * chunk, chunk)
+
+    def remote(src, dst, send, recv, device):
+        return pltpu.make_async_remote_copy(
+            src_ref=src, dst_ref=dst, send_sem=send, recv_sem=recv, device_id=device, device_id_type=MESH
+        )
+
+    def wq_copy(s):
+        k = pl.ds(pl.multiple_of(s * width, width), width)
+        return pltpu.make_async_copy(wq_hbm.at[0, k], wq.at[k], wq_sem.at[s])
+
+    def wkv_copy(s):
+        k = pl.ds(pl.multiple_of(s * width, width), width)
+        return pltpu.make_async_copy(wkv_hbm.at[0, k], wkv.at[k], wkv_sem.at[s])
+
+    def wo_copy(s):
+        a = pl.ds(pl.multiple_of(s * att_width, att_width), att_width)
+        return pltpu.make_async_copy(wo_hbm.at[0, a], wo.at[a], wo_sem.at[s])
+
+    def token_copy(i):
+        return pltpu.make_async_copy(tokens_hbm.at[rows(i)], stream.at[t, rows(i)], token_sem.at[i])
+
+    def y_copy(i, c):
+        part = stream.at[t, rows(i), cols(c)]
+        return remote(part, part, y_send.at[i, c], y_recv.at[i, c], {"tp": far})
+
+    def d_copy(i, c):
+        part = stream.at[t, rows(i), cols(c)]
+        return remote(part, part, d_send.at[i, c], d_recv.at[i, c], {"tp": near})
+
+    def r_copy(i, c):
+        part = stream.at[far, rows(i), cols(c)]
+        return remote(part, part, r_send.at[i, c], r_recv.at[i, c], {"tp": near})
+
+    def z_copy(i, c):
+        part = stream.at[t, rows(i), cols(c)]
+        return remote(part, part, z_send.at[i, c], z_recv.at[i, c], {"pp": jnp.minimum(sec + 1, last)})
+
+    def ay_copy(i):
+        part = attended.at[t, rows(i)]
+        return remote(part, part, ay_send.at[i], ay_recv.at[i], {"tp": far})
+
+    def ad_copy(i):
+        part = attended.at[t, rows(i)]
+        return remote(part, part, ad_send.at[i], ad_recv.at[i], {"tp": near})
+
+    def ar_copy(i):
+        part = attended.at[far, rows(i)]
+        return remote(part, part, ar_send.at[i], ar_recv.at[i], {"tp": near})
+
+    def h_copy(i):
+        return remote(
+            stream.at[t, rows(i)],
+            landed.at[rows(i % per_section)],
+            h_send.at[i],
+            h_recv.at[i % per_section],
+            {"pp": i // per_section},
+        )
+
+    def k_copy(kind):
+        which, to = ((t, far), (t, near), (far, near))[kind]
+        return remote(keyval.at[which], keyval.at[which], k_send.at[kind], k_recv.at[kind], {"tp": to})
+
+    def gain_copy(kind):
+        return remote(gain_ref, gains.at[t], gain_send.at[kind], gain_recv.at[kind], {"tp": (near, far, cross)[kind]})
+
+    @pl.when(sec == 0)
+    def _():
+        for i in range(M):
+            token_copy(i).start()
+
+    for s in sources:
+        wq_copy(s).start()
+        wkv_copy(s).start()
+    for s in sources:
+        wo_copy(s).start()
+
+    barrier = pltpu.get_barrier_semaphore()
+    for peer in (near, far, cross):
+        pl.semaphore_signal(barrier, inc=1, device_id={"tp": peer}, device_id_type=MESH)
+    for step in range(1, pp_size):
+        pl.semaphore_signal(barrier, inc=1, device_id={"pp": (sec + step) % pp_size}, device_id_type=MESH)
+    pl.semaphore_wait(barrier, 3 + pp_size - 1)
+
+    for kind in range(3):
+        gain_copy(kind).start()
+    keyval[t] = jnp.zeros((total_rows, kv_width), jnp.bfloat16)
+    gains[t] = gain_ref[...]
+
+    def forward(i, c):
+        @pl.when(sec == 0)
+        def _():
+            if c == 0:
+                token_copy(i).wait()
+
+        @pl.when(sec > 0)
+        def _():
+            z_copy(i, c).wait_recv()
+
+        y_copy(i, c).start()
+        d_copy(i, c).start()
+
+    def take(i, s, k0, kn, first):
+        x = stream[s, rows(i), pl.ds(k0, kn)].astype(jnp.float32)
+        sq = x * x
+        part = sq[:, :LANES]
+        for j in range(1, kn // LANES):
+            part = part + sq[:, j * LANES : (j + 1) * LANES]
+        squares[...] = part if first else squares[...] + part
+        g = gains[s, :, pl.ds(k0, kn)].astype(jnp.float32)
+        scaled[:, :kn] = (x * g).astype(jnp.bfloat16)
+        y = scaled[:, :kn]
+        k = pl.ds(pl.multiple_of(s * width + k0, chunk), kn)
+        for w, lo, hi in ((wq, 0, q_width), (wkv, q_width, q_width + kv_width)):
+            add = jnp.dot(y, w[k, :], preferred_element_type=jnp.float32)
+            acc[:, lo:hi] = add if first else acc[:, lo:hi] + add
+
+    def project(i):
+        def arrived(s):
+            @pl.when(i == 0)
+            def _():
+                wq_copy(s).wait()
+                wkv_copy(s).wait()
+
+        arrived(t)
+        take(i, t, 0, width, True)
+        arrived(near)
+        for c in range(C):
+            d_copy(i, c).wait_recv()
+        take(i, near, 0, width, False)
+        for c in range(C):
+            y_copy(i, c).wait_recv()
+            r_copy(i, c).start()
+            if c == 0:
+                arrived(far)
+            take(i, far, c * chunk, chunk, False)
+        arrived(cross)
+        for c in range(C):
+            r_copy(i, c).wait_recv()
+            take(i, cross, c * chunk, chunk, False)
+
+    def attend(i):
+        mean_sq = jnp.sum(squares[...], axis=1, keepdims=True) / model_width
+        scale = lax.rsqrt(mean_sq + eps_norm)
+        q = (acc[:, :q_width] * scale).astype(jnp.bfloat16)
+        keyval[t, rows(i)] = (acc[:, q_width:] * scale).astype(jnp.bfloat16)
+        q_pos = i * R + lax.broadcasted_iota(jnp.int32, (R, total_rows), 0)
+        k_pos = lax.broadcasted_iota(jnp.int32, (R, total_rows), 1)
+        kept = (k_pos <= q_pos) & (seg_row_ref[...] == seg_col_ref[rows(i)])
+        bias = jnp.where(kept, 0.0, -1e30).astype(jnp.float32)
+        held = kv_width // (2 * HEAD_SIZE)
+        per_kv = q_width // HEAD_SIZE // held
+        for g in range(held):
+            at = g * 2 * HEAD_SIZE
+            keys = keyval[t, :, at : at + HEAD_SIZE]
+            values = keyval[t, :, at + HEAD_SIZE : at + 2 * HEAD_SIZE]
+            heads = range(g * per_kv, (g + 1) * per_kv)
+            qg = jnp.concatenate([q[:, j * HEAD_SIZE : (j + 1) * HEAD_SIZE] for j in heads], axis=0)
+            s = lax.dot_general(qg, keys, (((1,), (1,)), ((), ())), preferred_element_type=jnp.float32)
+            s = s.reshape(per_kv, R, total_rows) * score_scale + bias[None]
+            s = s.reshape(per_kv * R, total_rows)
+            raised = jnp.exp(s - jnp.max(s, axis=-1, keepdims=True))
+            mass = jnp.sum(raised, axis=-1, keepdims=True)
+            mixed = jnp.dot(raised.astype(jnp.bfloat16), values, preferred_element_type=jnp.float32) / mass
+            mixed = mixed.astype(jnp.bfloat16)
+            for n, j in enumerate(heads):
+                attended[t, rows(i), j * HEAD_SIZE : (j + 1) * HEAD_SIZE] = mixed[n * R : (n + 1) * R]
+        ay_copy(i).start()
+        ad_copy(i).start()
+
+    def out_rows(s):
+        return pl.ds(pl.multiple_of(s * att_width, att_width), att_width)
+
+    def outputs(i):
+        def arrived(s):
+            @pl.when(i == 0)
+            def _():
+                wo_copy(s).wait()
+
+        arrived(t)
+        proj[...] = jnp.dot(attended[t, rows(i)], wo[out_rows(t), :], preferred_element_type=jnp.float32)
+        ad_copy(i).wait_recv()
+        arrived(near)
+        proj[...] += jnp.dot(attended[near, rows(i)], wo[out_rows(near), :], preferred_element_type=jnp.float32)
+        ay_copy(i).wait_recv()
+        ar_copy(i).start()
+        arrived(far)
+        proj[...] += jnp.dot(attended[far, rows(i)], wo[out_rows(far), :], preferred_element_type=jnp.float32)
+        for c in range(C):
+            y_copy(i, c).wait_send()
+            d_copy(i, c).wait_send()
+        ar_copy(i).wait_recv()
+        arrived(cross)
+        for c in range(C):
+            add = jnp.dot(attended[cross, rows(i)], wo[out_rows(cross), cols(c)], preferred_element_type=jnp.float32)
+            whole = stream[t, rows(i), cols(c)].astype(jnp.float32) + (proj[:, cols(c)] + add)
+            stream[t, rows(i), cols(c)] = whole.astype(jnp.bfloat16)
+
+            @pl.when(sec < last)
+            def _():
+                z_copy(i, c).start()
+
+        @pl.when((sec == last) & (i // per_section < last))
+        def _():
+            h_copy(i).start()
+
+    for c in range(C):
+        forward(0, c)
+    for kind in range(3):
+        gain_copy(kind).wait_recv()
+
+    def one(i, carry):
+        project(i)
+        attend(i)
+
+        @pl.when(i + 1 < M)
+        def _():
+            for c in range(C):
+                forward(i + 1, c)
+
+        outputs(i)
+        return carry
+
+    lax.fori_loop(0, M, one, 0)
+
+    k_copy(0).start()
+    k_copy(1).start()
+
+    @pl.when(sec < last)
+    def _():
+        for n in range(per_section):
+            h_copy(n).wait_recv()
+        done = pltpu.make_async_copy(landed, hidden_hbm, out_sem.at[0])
+        done.start()
+        done.wait()
+
+    @pl.when(sec == last)
+    def _():
+        done = pltpu.make_async_copy(
+            stream.at[t, pl.ds((M - per_section) * R, per_section * R)], hidden_hbm, out_sem.at[0]
+        )
+        done.start()
+        done.wait()
+
+    k_copy(0).wait_recv()
+    k_copy(2).start()
+    k_copy(1).wait_recv()
+    k_copy(2).wait_recv()
+    cache_rows = cache.shape[0]
+    block = cache_rows // 4
+    held = kv_width // (2 * HEAD_SIZE)
+
+    def assemble(b, carry):
+        start = pl.multiple_of(b * block, block)
+        slot = t * cache_rows + start + lax.broadcasted_iota(jnp.int32, (block, total_rows), 0)
+        total = jnp.zeros((block, 2 * HEAD_SIZE), jnp.float32)
+        for s in range(4):
+            for g in range(held):
+                head = s * held + g
+                onehot = jnp.where(ids_ref[head : head + 1, :] == slot, 1.0, 0.0).astype(jnp.bfloat16)
+                pages = keyval[s, :, g * 2 * HEAD_SIZE : (g + 1) * 2 * HEAD_SIZE]
+                total = total + jnp.dot(onehot, pages, preferred_element_type=jnp.float32)
+        cache[pl.ds(start, block), :] = total.astype(jnp.bfloat16)
+        return carry
+
+    lax.fori_loop(0, 4, assemble, 0)
+    stored = pltpu.make_async_copy(cache, cache_hbm, out_sem.at[1])
+    stored.start()
+
+    def drain(i, carry):
+        for c in range(C):
+            r_copy(i, c).wait_send()
+
+            @pl.when(sec < last)
+            def _():
+                z_copy(i, c).wait_send()
+
+        ay_copy(i).wait_send()
+        ad_copy(i).wait_send()
+        ar_copy(i).wait_send()
+
+        @pl.when((sec == last) & (i // per_section < last))
+        def _():
+            h_copy(i).wait_send()
+
+        return carry
+
+    lax.fori_loop(0, M, drain, 0)
+    for kind in range(3):
+        k_copy(kind).wait_send()
+        gain_copy(kind).wait_send()
+    stored.wait()
+
+
+def kernel_body(tokens, gain, q_weight, kv_weight, out_weight, page_table, segment_ids):
+    pp_size = lax.axis_size("pp")
+    total_rows, width = tokens.shape
+    M = 2 * pp_size
+    R = total_rows // M
+    q_width, kv_width = q_weight.shape[2], kv_weight.shape[2]
+    att_all = out_weight.shape[1]
+    att_width = att_all // 4
+    heads, blocks = page_table.shape[1:]
+    cache_rows = heads * total_rows // 4
+    token_in_page = jnp.arange(total_rows, dtype=jnp.int32) % PAGE_TOKENS
+    ids = jnp.repeat(page_table[0], PAGE_TOKENS, axis=1) * PAGE_TOKENS + token_in_page[None, :]
+    any_spec = pl.BlockSpec(memory_space=pl.ANY)
+    vmem_spec = pl.BlockSpec(memory_space=pltpu.VMEM)
+    dma = pltpu.SemaphoreType.DMA
+    C = STREAM_CHUNKS
+    bf16, f32 = jnp.bfloat16, jnp.float32
+    hidden, cache = pl.pallas_call(
+        functools.partial(section_kernel, R, M, pp_size),
+        out_shape=(
+            jax.ShapeDtypeStruct((total_rows // pp_size, width), bf16),
+            jax.ShapeDtypeStruct((cache_rows, 2 * HEAD_SIZE), bf16),
+        ),
+        in_specs=[any_spec, vmem_spec, any_spec, any_spec, any_spec, vmem_spec, vmem_spec, vmem_spec],
+        out_specs=(any_spec, any_spec),
+        scratch_shapes=[
+            pltpu.VMEM((4 * width, q_width), bf16),
+            pltpu.VMEM((4 * width, kv_width), bf16),
+            pltpu.VMEM((att_all, width), bf16),
+            pltpu.VMEM((4, total_rows, width), bf16),
+            pltpu.VMEM((4, total_rows, att_width), bf16),
+            pltpu.VMEM((4, total_rows, kv_width), bf16),
+            pltpu.VMEM((4, 1, width), bf16),
+            pltpu.VMEM((R, width), bf16),
+            pltpu.VMEM((R, q_width + kv_width), f32),
+            pltpu.VMEM((R, width), f32),
+            pltpu.VMEM((R, LANES), f32),
+            pltpu.VMEM((total_rows // pp_size, width), bf16),
+            pltpu.VMEM((cache_rows, 2 * HEAD_SIZE), bf16),
+            dma((4,)),
+            dma((4,)),
+            dma((4,)),
+            dma((M,)),
+            dma((3,)),
+            dma((3,)),
+            dma((M, C)),
+            dma((M, C)),
+            dma((M, C)),
+            dma((M, C)),
+            dma((M, C)),
+            dma((M, C)),
+            dma((M, C)),
+            dma((M, C)),
+            dma((M,)),
+            dma((M,)),
+            dma((M,)),
+            dma((M,)),
+            dma((M,)),
+            dma((M,)),
+            dma((3,)),
+            dma((3,)),
+            dma((M,)),
+            dma((M // pp_size,)),
+            dma((2,)),
+        ],
+        compiler_params=pltpu.CompilerParams(
+            collective_id=0, has_side_effects=True, vmem_limit_bytes=67043328
+        ),
+    )(
+        tokens,
+        gain,
+        q_weight,
+        kv_weight,
+        out_weight,
+        ids,
+        segment_ids[None, :],
+        segment_ids[:, None],
+    )
+    pages = cache.reshape(1, cache_rows // PAGE_TOKENS, PAGE_TOKENS, 2 * HEAD_SIZE)
+    return hidden, pages
+
+
+def chosen_body(tokens, gain, q_weight, kv_weight, out_weight, page_table, segment_ids):
+    whole_heads = kv_weight.shape[2] % (2 * HEAD_SIZE) == 0
+    rows_fit = tokens.shape[0] % (32 * lax.axis_size("pp")) == 0
+    if lax.axis_size("tp") == 4 and whole_heads and rows_fit:
+        return kernel_body(tokens, gain, q_weight, kv_weight, out_weight, page_table, segment_ids)
+    return body(tokens, gain, q_weight, kv_weight, out_weight, page_table, segment_ids)
+
+
 def solution(mesh):
     placed = (
         P("grp", "tp"),
@@ -163,7 +631,7 @@
         P("grp"),
     )
     return jax.shard_map(
-        body,
+        chosen_body,
         mesh=mesh,
         in_specs=placed,
         out_specs=(P(("grp", "pp"), "tp"), P("pp", ("grp", "tp"), None, None)),

time: 648 us -> 212 us (0.33); the launches traced: 639 us -> 212 us
  waiting for transfers between devices: 364 us -> 0 us
  Pallas kernels: 0 us -> 204 us
  matrix products: 184 us -> 0 us
  other arithmetic: 27.1 us -> 1.32 us
  local copies, waits for them, and re-layouts: 26.5 us -> 5.61 us
  starting transfers between devices: 16.3 us -> 0 us
  between operations: 15.4 us -> 0.65 us
    all_gather x15 -> x0, waiting for transfers between devices: 270 us -> none  [the longest x7 155 us: one_step(): lax.all_gather(current, 'tp', axis=1, tiled=True).astype(jnp.float32)]
    pallas_call x0 -> x1, Pallas kernels: none -> 204 us  [kernel_body(): pl.pallas_call(functools.partial(section_kernel, R, M, pp_size), out_shap...]
    dot_general x31 -> x0, matrix products: 172 us -> none  [the longest x7 59.3 us: add_outputs(): return jnp.dot(block_cols, w_output, preferred_element_type=jnp.float32)]
    ppermute x9 -> x0, waiting for transfers between devices: 93.7 us -> none  [the longest x6 82.7 us: shifted(): return lax.ppermute(x, axis, pairs)]
    reduce_sum x7 -> x0, other arithmetic: 15.6 us -> none  [one_step(): jnp.sum(whole_rows * whole_rows, axis=1, keepdims=True) / MODEL_WIDTH]
    ppermute x9 -> x0, starting transfers between devices: 14.1 us -> none  [the longest x6 8.11 us: shifted(): return lax.ppermute(x, axis, pairs)]
    sub x7 -> x0, matrix products: 11.6 us -> none  [one_step(): raised = jnp.exp(scores - row_max)]
    select_n x8 -> x1, other arithmetic: 8.5 us -> 0.01 us  [kernel_body(): token_in_page = jnp.arange(total_rows, dtype=jnp.int32) % PAGE_TOKENS]
  transfers between devices with their start and end apart: 24 -> 0, of which waited for: 22 -> 0; matrix products, arithmetic and copies ran while one was open for 2% -> 0% of each run, Pallas kernels for 0% -> 0%
where the time goes in v1:
time: 212 us
  Pallas kernels  204 us (96%)
  local copies, waits for them, and re-layouts  5.61 us (3%)
    pallas_call x1, Pallas kernels, kernel_body(): pl.pallas_call(functools.partial(section_kernel, R, M, pp_size), out_shap...  204 us

profile of v1, /device:TPU:27, one launch (start us, length us, event | category | flops | bytes accessed | tf_op | source)
XLA Modules:
  0.0 211.7 jit_solution(1896184919476956434)
XLA Ops:
  0.6 0.7 multiply_bitcast_fusion
  1.3 0.1 copy.9
  1.5 0.1 copy.10
  1.6 0.6 broadcast_add_fusion.ids_ref
  2.2 1.5 copy.11.seg_col_ref
  3.7 204.1 %shard_map.86 = (bf16[128,2048]{1,0:T(8,128)(2,1)}, bf16[1024,256]{1,0:T(8,128)(2,1)}) custom-call(bf16[512,2048]{1,0:T(8,128)(2,1)} %tokens_hbm.1, bf16[1,2048]{1,0:T(2,128)(2,1)} %gain_ref.1, bf16[1,8192,1024]{2,1,0:T(8,128)(2,1)} %wq_hbm.1, bf16[1,8192,512]{2,1,0:T(8,128)(2,1)} %wkv_hbm.1, bf16[1,4096,2048]{2,1,0:T(8,128)(2,1)} %wo_hbm.1, ...), custom_call_target="tpu_custom_call" | custom-call | tf_op jit(solution)/shard_map/pallas_call | solution.py:550
  207.9 2.0 reshape.21
  209.8 1.9 copy.13
  (2 shorter events, 0.0 us)

commit v2 on v1

--- a/solution.py
+++ b/solution.py
@@ -157,7 +157,7 @@
 
 MESH = pl.DeviceIdType.MESH
 LANES = 128
-STREAM_CHUNKS = 2
+STREAM_CHUNKS = 4
 
 
 def section_kernel(
@@ -169,9 +169,8 @@
     wq_hbm,
     wkv_hbm,
     wo_hbm,
-    ids_ref,
+    table_ref,
     seg_row_ref,
-    seg_col_ref,
     hidden_hbm,
     cache_hbm,
     wq,
@@ -181,12 +180,13 @@
     attended,
     keyval,
     gains,
-    scaled,
     acc,
     proj,
     squares,
     landed,
     cache,
+    seg_col,
+    ids,
     wq_sem,
     wkv_sem,
     wo_sem,
@@ -295,9 +295,10 @@
             {"pp": i // per_section},
         )
 
-    def k_copy(kind):
+    def k_copy(kind, i):
         which, to = ((t, far), (t, near), (far, near))[kind]
-        return remote(keyval.at[which], keyval.at[which], k_send.at[kind], k_recv.at[kind], {"tp": to})
+        part = keyval.at[which, rows(i)]
+        return remote(part, part, k_send.at[kind, i], k_recv.at[kind, i], {"tp": to})
 
     def gain_copy(kind):
         return remote(gain_ref, gains.at[t], gain_send.at[kind], gain_recv.at[kind], {"tp": (near, far, cross)[kind]})
@@ -318,12 +319,21 @@
         pl.semaphore_signal(barrier, inc=1, device_id={"tp": peer}, device_id_type=MESH)
     for step in range(1, pp_size):
         pl.semaphore_signal(barrier, inc=1, device_id={"pp": (sec + step) % pp_size}, device_id_type=MESH)
-    pl.semaphore_wait(barrier, 3 + pp_size - 1)
-
-    for kind in range(3):
-        gain_copy(kind).start()
+
+    for n in range(total_rows // LANES):
+        across = jnp.broadcast_to(seg_row_ref[:, n * LANES : (n + 1) * LANES].astype(jnp.float32), (LANES, LANES))
+        seg_col[n * LANES : (n + 1) * LANES, :] = across.T
+    heads, blocks = table_ref.shape[1:]
+    spread = lax.broadcasted_iota(jnp.int32, (blocks, total_rows), 1) // PAGE_TOKENS
+    spread = jnp.where(spread == lax.broadcasted_iota(jnp.int32, (blocks, total_rows), 0), 1.0, 0.0).astype(jnp.bfloat16)
+    table = table_ref[0]
+    upper = jnp.dot((table // 256).astype(jnp.float32).astype(jnp.bfloat16), spread, preferred_element_type=jnp.float32)
+    lower = jnp.dot((table % 256).astype(jnp.float32).astype(jnp.bfloat16), spread, preferred_element_type=jnp.float32)
+    in_page = lax.broadcasted_iota(jnp.int32, (heads, total_rows), 1) % PAGE_TOKENS
+    ids[...] = (upper * 256.0 + lower) * PAGE_TOKENS + in_page.astype(jnp.float32)
     keyval[t] = jnp.zeros((total_rows, kv_width), jnp.bfloat16)
     gains[t] = gain_ref[...]
+    pl.semaphore_wait(barrier, 3 + pp_size - 1)
 
     def forward(i, c):
         @pl.when(sec == 0)
@@ -338,54 +348,47 @@
         y_copy(i, c).start()
         d_copy(i, c).start()
 
-    def take(i, s, k0, kn, first):
-        x = stream[s, rows(i), pl.ds(k0, kn)].astype(jnp.float32)
-        sq = x * x
+    def relay(i, c):
+        y_copy(i, c).wait_recv()
+        r_copy(i, c).start()
+
+    def take(i, s):
+        x = stream[s, rows(i)]
+        wide = x.astype(jnp.float32)
+        sq = wide * wide
         part = sq[:, :LANES]
-        for j in range(1, kn // LANES):
+        for j in range(1, width // LANES):
             part = part + sq[:, j * LANES : (j + 1) * LANES]
-        squares[...] = part if first else squares[...] + part
-        g = gains[s, :, pl.ds(k0, kn)].astype(jnp.float32)
-        scaled[:, :kn] = (x * g).astype(jnp.bfloat16)
-        y = scaled[:, :kn]
-        k = pl.ds(pl.multiple_of(s * width + k0, chunk), kn)
-        for w, lo, hi in ((wq, 0, q_width), (wkv, q_width, q_width + kv_width)):
-            add = jnp.dot(y, w[k, :], preferred_element_type=jnp.float32)
-            acc[:, lo:hi] = add if first else acc[:, lo:hi] + add
-
-    def project(i):
-        def arrived(s):
-            @pl.when(i == 0)
-            def _():
-                wq_copy(s).wait()
-                wkv_copy(s).wait()
-
-        arrived(t)
-        take(i, t, 0, width, True)
-        arrived(near)
-        for c in range(C):
-            d_copy(i, c).wait_recv()
-        take(i, near, 0, width, False)
-        for c in range(C):
-            y_copy(i, c).wait_recv()
-            r_copy(i, c).start()
-            if c == 0:
-                arrived(far)
-            take(i, far, c * chunk, chunk, False)
-        arrived(cross)
-        for c in range(C):
-            r_copy(i, c).wait_recv()
-            take(i, cross, c * chunk, chunk, False)
+        y = x * gains[s]
+        k = pl.ds(pl.multiple_of(s * width, width), width)
+        return (
+            part,
+            jnp.dot(y, wq[k, :], preferred_element_type=jnp.float32),
+            jnp.dot(y, wkv[k, :], preferred_element_type=jnp.float32),
+        )
+
+    def near_part(i):
+        a, b = take(i, t), take(i, near)
+        squares[...] = a[0] + b[0]
+        acc[:, :q_width] = a[1] + b[1]
+        acc[:, q_width:] = a[2] + b[2]
+
+    def far_part(i):
+        a = take(i, far)
+        squares[...] += a[0]
+        acc[:, :q_width] += a[1]
+        acc[:, q_width:] += a[2]
 
     def attend(i):
-        mean_sq = jnp.sum(squares[...], axis=1, keepdims=True) / model_width
+        a = take(i, cross)
+        mean_sq = jnp.sum(squares[...] + a[0], axis=1, keepdims=True) / model_width
         scale = lax.rsqrt(mean_sq + eps_norm)
-        q = (acc[:, :q_width] * scale).astype(jnp.bfloat16)
-        keyval[t, rows(i)] = (acc[:, q_width:] * scale).astype(jnp.bfloat16)
+        q = ((acc[:, :q_width] + a[1]) * scale).astype(jnp.bfloat16)
+        keyval[t, rows(i)] = ((acc[:, q_width:] + a[2]) * scale).astype(jnp.bfloat16)
         q_pos = i * R + lax.broadcasted_iota(jnp.int32, (R, total_rows), 0)
         k_pos = lax.broadcasted_iota(jnp.int32, (R, total_rows), 1)
-        kept = (k_pos <= q_pos) & (seg_row_ref[...] == seg_col_ref[rows(i)])
-        bias = jnp.where(kept, 0.0, -1e30).astype(jnp.float32)
+        same = seg_row_ref[...].astype(jnp.float32) == seg_col[rows(i), 0:1]
+        bias = jnp.where((k_pos <= q_pos) & same, 0.0, -1e30).astype(jnp.float32)
         held = kv_width // (2 * HEAD_SIZE)
         per_kv = q_width // HEAD_SIZE // held
         for g in range(held):
@@ -406,102 +409,206 @@
         ay_copy(i).start()
         ad_copy(i).start()
 
+        @pl.when(sec == last)
+        def _():
+            k_copy(0, i).start()
+            k_copy(1, i).start()
+
     def out_rows(s):
         return pl.ds(pl.multiple_of(s * att_width, att_width), att_width)
 
-    def outputs(i):
-        def arrived(s):
-            @pl.when(i == 0)
-            def _():
-                wo_copy(s).wait()
-
-        arrived(t)
-        proj[...] = jnp.dot(attended[t, rows(i)], wo[out_rows(t), :], preferred_element_type=jnp.float32)
+    def from_att(i, s, at):
+        return jnp.dot(attended[s, rows(i)], wo[out_rows(s), at], preferred_element_type=jnp.float32)
+
+    def near_out(i):
         ad_copy(i).wait_recv()
-        arrived(near)
-        proj[...] += jnp.dot(attended[near, rows(i)], wo[out_rows(near), :], preferred_element_type=jnp.float32)
+        every = slice(None)
+        proj[...] = from_att(i, t, every) + from_att(i, near, every)
+
+    def relay_att(i):
         ay_copy(i).wait_recv()
         ar_copy(i).start()
-        arrived(far)
-        proj[...] += jnp.dot(attended[far, rows(i)], wo[out_rows(far), :], preferred_element_type=jnp.float32)
+
+    def far_out(i):
         for c in range(C):
             y_copy(i, c).wait_send()
             d_copy(i, c).wait_send()
         ar_copy(i).wait_recv()
-        arrived(cross)
-        for c in range(C):
-            add = jnp.dot(attended[cross, rows(i)], wo[out_rows(cross), cols(c)], preferred_element_type=jnp.float32)
-            whole = stream[t, rows(i), cols(c)].astype(jnp.float32) + (proj[:, cols(c)] + add)
-            stream[t, rows(i), cols(c)] = whole.astype(jnp.bfloat16)
+        wide = 2 * chunk
+        for n in range(C // 2):
+            at = pl.ds(n * wide, wide)
+            add = from_att(i, far, at) + from_att(i, cross, at)
+            whole = stream[t, rows(i), at].astype(jnp.float32) + (proj[:, at] + add)
+            stream[t, rows(i), at] = whole.astype(jnp.bfloat16)
 
             @pl.when(sec < last)
             def _():
-                z_copy(i, c).start()
+                z_copy(i, 2 * n).start()
+                z_copy(i, 2 * n + 1).start()
 
         @pl.when((sec == last) & (i // per_section < last))
         def _():
             h_copy(i).start()
 
+    cache_rows = cache.shape[0]
+    block = cache_rows // 4
+    held = kv_width // (2 * HEAD_SIZE)
+    half = total_rows // 2
+
+    def assemble(n):
+        at = slice(n * half, (n + 1) * half)
+
+        def one_block(b, carry):
+            start = pl.multiple_of(b * block, block)
+            row = lax.broadcasted_iota(jnp.int32, (block, half), 0)
+            row = (row + t * cache_rows + start).astype(jnp.float32)
+            total = jnp.zeros((block, 2 * HEAD_SIZE), jnp.float32)
+            for s in range(4):
+                for g in range(held):
+                    head = s * held + g
+                    onehot = jnp.where(ids[head : head + 1, at] == row, 1.0, 0.0).astype(jnp.bfloat16)
+                    pages = keyval[s, at, g * 2 * HEAD_SIZE : (g + 1) * 2 * HEAD_SIZE]
+                    total = total + jnp.dot(onehot, pages, preferred_element_type=jnp.float32)
+            if n == 1:
+                total = total + cache[pl.ds(start, block), :].astype(jnp.float32)
+            cache[pl.ds(start, block), :] = total.astype(jnp.bfloat16)
+            return carry
+
+        lax.fori_loop(0, 4, one_block, 0)
+
+    def relay_pages(i):
+        k_copy(0, i).wait_recv()
+        k_copy(2, i).start()
+
+    def pages_in(lo, hi):
+        def one_mb(i, carry):
+            k_copy(1, i).wait_recv()
+            k_copy(2, i).wait_recv()
+            return carry
+
+        lax.fori_loop(lo, hi, one_mb, 0)
+
+    for kind in range(3):
+        gain_copy(kind).start()
     for c in range(C):
         forward(0, c)
+    wq_copy(t).wait()
+    wkv_copy(t).wait()
+    wq_copy(near).wait()
+    wkv_copy(near).wait()
     for kind in range(3):
         gain_copy(kind).wait_recv()
+    for c in range(C):
+        d_copy(0, c).wait_recv()
+    near_part(0)
+    for c in range(C):
+        relay(0, c)
+    first, final = sec == 0, sec == last
+    middle = (sec > 0) & (sec < last)
+
+    @pl.when(first | final)
+    def _():
+        for c in range(C // 2):
+            forward(1, c)
+
+    wq_copy(far).wait()
+    wkv_copy(far).wait()
+    far_part(0)
+    wq_copy(cross).wait()
+    wkv_copy(cross).wait()
+
+    @pl.when(middle)
+    def _():
+        for c in range(C // 2):
+            forward(1, c)
+
+    for c in range(C // 2, C):
+        forward(1, c)
+    for c in range(C):
+        r_copy(0, c).wait_recv()
+    attend(0)
+    for s in sources:
+        wo_copy(s).wait()
 
     def one(i, carry):
-        project(i)
-        attend(i)
-
-        @pl.when(i + 1 < M)
+        def ahead(where, *chunks):
+            @pl.when((i + 2 < M) & where)
+            def _():
+                for c in chunks:
+                    forward(i + 2, c)
+
+        for c in range(C):
+            d_copy(i + 1, c).wait_recv()
+        near_part(i + 1)
+        ahead(first, 0, 1)
+        ahead(sec > 0, 0)
+        near_out(i)
+        ahead(middle, 1)
+        ahead(final, 1, 2)
+        for c in range(C):
+            relay(i + 1, c)
+        far_part(i + 1)
+        ahead(sec < last, 2)
+        ahead(final, 3)
+        relay_att(i)
+        ahead(first, 3)
+        for c in range(C):
+            r_copy(i + 1, c).wait_recv()
+        attend(i + 1)
+        ahead(middle, 3)
+
+        @pl.when(sec == last)
         def _():
-            for c in range(C):
-                forward(i + 1, c)
-
-        outputs(i)
+            relay_pages(i)
+
+        far_out(i)
         return carry
 
-    lax.fori_loop(0, M, one, 0)
-
-    k_copy(0).start()
-    k_copy(1).start()
+    lax.fori_loop(0, M - 1, one, 0)
+    near_out(M - 1)
+
+    @pl.when(sec == last)
+    def _():
+        pages_in(0, M // 2)
+        assemble(0)
+
+    relay_att(M - 1)
+
+    @pl.when(sec == last)
+    def _():
+        relay_pages(M - 1)
+
+    far_out(M - 1)
 
     @pl.when(sec < last)
     def _():
+        def send_pages(i, carry):
+            k_copy(0, i).start()
+            k_copy(1, i).start()
+            return carry
+
+        def pass_pages(i, carry):
+            relay_pages(i)
+            return carry
+
+        lax.fori_loop(0, M, send_pages, 0)
+        lax.fori_loop(0, M, pass_pages, 0)
+        pages_in(0, M // 2)
+        assemble(0)
         for n in range(per_section):
             h_copy(n).wait_recv()
         done = pltpu.make_async_copy(landed, hidden_hbm, out_sem.at[0])
         done.start()
         done.wait()
 
+    mine = stream.at[t, pl.ds((M - per_section) * R, per_section * R)]
+
     @pl.when(sec == last)
     def _():
-        done = pltpu.make_async_copy(
-            stream.at[t, pl.ds((M - per_section) * R, per_section * R)], hidden_hbm, out_sem.at[0]
-        )
-        done.start()
-        done.wait()
-
-    k_copy(0).wait_recv()
-    k_copy(2).start()
-    k_copy(1).wait_recv()
-    k_copy(2).wait_recv()
-    cache_rows = cache.shape[0]
-    block = cache_rows // 4
-    held = kv_width // (2 * HEAD_SIZE)
-
-    def assemble(b, carry):
-        start = pl.multiple_of(b * block, block)
-        slot = t * cache_rows + start + lax.broadcasted_iota(jnp.int32, (block, total_rows), 0)
-        total = jnp.zeros((block, 2 * HEAD_SIZE), jnp.float32)
-        for s in range(4):
-            for g in range(held):
-                head = s * held + g
-                onehot = jnp.where(ids_ref[head : head + 1, :] == slot, 1.0, 0.0).astype(jnp.bfloat16)
-                pages = keyval[s, :, g * 2 * HEAD_SIZE : (g + 1) * 2 * HEAD_SIZE]
-                total = total + jnp.dot(onehot, pages, preferred_element_type=jnp.float32)
-        cache[pl.ds(start, block), :] = total.astype(jnp.bfloat16)
-        return carry
-
-    lax.fori_loop(0, 4, assemble, 0)
+        pltpu.make_async_copy(mine, hidden_hbm, out_sem.at[0]).start()
+
+    pages_in(M // 2, M)
+    assemble(1)
     stored = pltpu.make_async_copy(cache, cache_hbm, out_sem.at[1])
     stored.start()
 
@@ -516,6 +623,8 @@
         ay_copy(i).wait_send()
         ad_copy(i).wait_send()
         ar_copy(i).wait_send()
+        for kind in range(3):
+            k_copy(kind, i).wait_send()
 
         @pl.when((sec == last) & (i // per_section < last))
         def _():
@@ -525,8 +634,12 @@
 
     lax.fori_loop(0, M, drain, 0)
     for kind in range(3):
-        k_copy(kind).wait_send()
         gain_copy(kind).wait_send()
+
+    @pl.when(sec == last)
+    def _():
+        pltpu.make_async_copy(mine, hidden_hbm, out_sem.at[0]).wait()
+
     stored.wait()
 
 
@@ -538,10 +651,8 @@
     q_width, kv_width = q_weight.shape[2], kv_weight.shape[2]
     att_all = out_weight.shape[1]
     att_width = att_all // 4
-    heads, blocks = page_table.shape[1:]
+    heads = page_table.shape[1]
     cache_rows = heads * total_rows // 4
-    token_in_page = jnp.arange(total_rows, dtype=jnp.int32) % PAGE_TOKENS
-    ids = jnp.repeat(page_table[0], PAGE_TOKENS, axis=1) * PAGE_TOKENS + token_in_page[None, :]
     any_spec = pl.BlockSpec(memory_space=pl.ANY)
     vmem_spec = pl.BlockSpec(memory_space=pltpu.VMEM)
     dma = pltpu.SemaphoreType.DMA
@@ -553,7 +664,7 @@
             jax.ShapeDtypeStruct((total_rows // pp_size, width), bf16),
             jax.ShapeDtypeStruct((cache_rows, 2 * HEAD_SIZE), bf16),
         ),
-        in_specs=[any_spec, vmem_spec, any_spec, any_spec, any_spec, vmem_spec, vmem_spec, vmem_spec],
+        in_specs=[any_spec, vmem_spec, any_spec, any_spec, any_spec, vmem_spec, vmem_spec],
         out_specs=(any_spec, any_spec),
         scratch_shapes=[
             pltpu.VMEM((4 * width, q_width), bf16),
@@ -563,12 +674,13 @@
             pltpu.VMEM((4, total_rows, att_width), bf16),
             pltpu.VMEM((4, total_rows, kv_width), bf16),
             pltpu.VMEM((4, 1, width), bf16),
-            pltpu.VMEM((R, width), bf16),
             pltpu.VMEM((R, q_width + kv_width), f32),
             pltpu.VMEM((R, width), f32),
             pltpu.VMEM((R, LANES), f32),
             pltpu.VMEM((total_rows // pp_size, width), bf16),
             pltpu.VMEM((cache_rows, 2 * HEAD_SIZE), bf16),
+            pltpu.VMEM((total_rows, LANES), f32),
+            pltpu.VMEM((heads, total_rows), f32),
             dma((4,)),
             dma((4,)),
             dma((4,)),
@@ -589,8 +701,8 @@
             dma((M,)),
             dma((M,)),
             dma((M,)),
-            dma((3,)),
-            dma((3,)),
+            dma((3, M)),
+            dma((3, M)),
             dma((M,)),
             dma((M // pp_size,)),
             dma((2,)),
@@ -604,9 +716,8 @@
         q_weight,
         kv_weight,
         out_weight,
-        ids,
+        page_table,
         segment_ids[None, :],
-        segment_ids[:, None],
     )
     pages = cache.reshape(1, cache_rows // PAGE_TOKENS, PAGE_TOKENS, 2 * HEAD_SIZE)
     return hidden, pages

time: 212 us -> 186 us (0.88)
  Pallas kernels: 204 us -> 182 us
    pallas_call x1, Pallas kernels: 204 us -> 182 us  [kernel_body(): pl.pallas_call(functools.partial(section_kernel, R, M, pp_size), out_shap...]
where the time goes in v2:
time: 186 us
  Pallas kernels  182 us (98%)
  local copies, waits for them, and re-layouts  3.84 us (2%)
    pallas_call x1, Pallas kernels, kernel_body(): pl.pallas_call(functools.partial(section_kernel, R, M, pp_size), out_shap...  182 us

profile of v2, /device:TPU:27, one launch (start us, length us, event | category | flops | bytes accessed | tf_op | source)
XLA Modules:
  0.0 186.0 jit_solution(7518656744520043492)
XLA Ops:
  0.6 181.5 %shard_map.86 = (bf16[128,2048]{1,0:T(8,128)(2,1)}, bf16[1024,256]{1,0:T(8,128)(2,1)}) custom-call(bf16[512,2048]{1,0:T(8,128)(2,1)} %tokens_hbm.1, bf16[1,2048]{1,0:T(2,128)(2,1)} %gain_ref.1, bf16[1,8192,1024]{2,1,0:T(8,128)(2,1)} %wq_hbm.1, bf16[1,8192,512]{2,1,0:T(8,128)(2,1)} %wkv_hbm.1, bf16[1,4096,2048]{2,1,0:T(8,128)(2,1)} %wo_hbm.1, ...), custom_call_target="tpu_custom_call" | custom-call | tf_op jit(solution)/shard_map/pallas_call | solution.py:661
  182.2 2.0 %reshape.7 = bf16[1,256,4,256]{3,2,1,0:T(4,128)(2,1)} reshape(bf16[1024,256]{1,0:T(8,128)(2,1)} %get-tuple-element.5) | data formatting | bytes 1048576 | tf_op jit(solution)/shard_map/reshape | solution.py:722
  184.1 1.9 %copy.10 = bf16[128,2048]{1,0:T(8,128)(2,1)} copy(bf16[128,2048]{1,0:T(8,128)(2,1)} %get-tuple-element.8) | data formatting | bytes 1048576

commit v3 on v2

--- a/solution.py
+++ b/solution.py
@@ -158,6 +158,7 @@
 MESH = pl.DeviceIdType.MESH
 LANES = 128
 STREAM_CHUNKS = 4
+MATMUL_ROWS = 128
 
 
 def section_kernel(
@@ -352,6 +353,12 @@
         y_copy(i, c).wait_recv()
         r_copy(i, c).start()
 
+    def product(x, w):
+        n = x.shape[0]
+        if 2 * n <= MATMUL_ROWS:
+            x = jnp.concatenate([x, x], axis=0)
+        return jnp.dot(x, w, preferred_element_type=jnp.float32)[:n]
+
     def take(i, s):
         x = stream[s, rows(i)]
         wide = x.astype(jnp.float32)
@@ -361,11 +368,7 @@
             part = part + sq[:, j * LANES : (j + 1) * LANES]
         y = x * gains[s]
         k = pl.ds(pl.multiple_of(s * width, width), width)
-        return (
-            part,
-            jnp.dot(y, wq[k, :], preferred_element_type=jnp.float32),
-            jnp.dot(y, wkv[k, :], preferred_element_type=jnp.float32),
-        )
+        return part, product(y, wq[k, :]), product(y, wkv[k, :])
 
     def near_part(i):
         a, b = take(i, t), take(i, near)
@@ -418,7 +421,7 @@
         return pl.ds(pl.multiple_of(s * att_width, att_width), att_width)
 
     def from_att(i, s, at):
-        return jnp.dot(attended[s, rows(i)], wo[out_rows(s), at], preferred_element_type=jnp.float32)
+        return product(attended[s, rows(i)], wo[out_rows(s), at])
 
     def near_out(i):
         ad_copy(i).wait_recv()

time: 186 us -> 182 us (0.978)
  Pallas kernels: 182 us -> 177 us
    pallas_call x1, Pallas kernels: 182 us -> 177 us  [kernel_body(): pl.pallas_call(functools.partial(section_kernel, R, M, pp_size), out_shap...]
where the time goes in v3:
time: 182 us
  Pallas kernels  177 us (97%)
  local copies, waits for them, and re-layouts  3.84 us (2%)
    pallas_call x1, Pallas kernels, kernel_body(): pl.pallas_call(functools.partial(section_kernel, R, M, pp_size), out_shap...  177 us

profile of v3, /device:TPU:27, one launch (start us, length us, event | category | flops | bytes accessed | tf_op | source)
XLA Modules:
  0.0 181.9 jit_solution(11799075726435034481)
XLA Ops:
  0.6 177.5 %shard_map.86 = (bf16[128,2048]{1,0:T(8,128)(2,1)}, bf16[1024,256]{1,0:T(8,128)(2,1)}) custom-call(bf16[512,2048]{1,0:T(8,128)(2,1)} %tokens_hbm.1, bf16[1,2048]{1,0:T(2,128)(2,1)} %gain_ref.1, bf16[1,8192,1024]{2,1,0:T(8,128)(2,1)} %wq_hbm.1, bf16[1,8192,512]{2,1,0:T(8,128)(2,1)} %wkv_hbm.1, bf16[1,4096,2048]{2,1,0:T(8,128)(2,1)} %wo_hbm.1, ...), custom_call_target="tpu_custom_call" | custom-call | tf_op jit(solution)/shard_map/pallas_call | solution.py:664
  178.1 2.0 %reshape.7 = bf16[1,256,4,256]{3,2,1,0:T(4,128)(2,1)} reshape(bf16[1024,256]{1,0:T(8,128)(2,1)} %get-tuple-element.5) | data formatting | bytes 1048576 | tf_op jit(solution)/shard_map/reshape | solution.py:725
  180.1 1.9 %copy.10 = bf16[128,2048]{1,0:T(8,128)(2,1)} copy(bf16[128,2048]{1,0:T(8,128)(2,1)} %get-tuple-element.8) | data formatting | bytes 1048576

commit v4 on v3

--- a/solution.py
+++ b/solution.py
@@ -210,9 +210,11 @@
     ar_recv,
     k_send,
     k_recv,
+    k_in,
     h_send,
     h_recv,
     out_sem,
+    cache_sem,
 ):
     R, M, C = rows_of_mb, micro_batches, STREAM_CHUNKS
     width = stream.shape[2]
@@ -261,45 +263,64 @@
 
     def y_copy(i, c):
         part = stream.at[t, rows(i), cols(c)]
-        return remote(part, part, y_send.at[i, c], y_recv.at[i, c], {"tp": far})
+        return remote(part, part, y_send.at[i], y_recv.at[i, c], {"tp": far})
 
     def d_copy(i, c):
         part = stream.at[t, rows(i), cols(c)]
-        return remote(part, part, d_send.at[i, c], d_recv.at[i, c], {"tp": near})
+        return remote(part, part, d_send.at[i], d_recv.at[i], {"tp": near})
 
     def r_copy(i, c):
         part = stream.at[far, rows(i), cols(c)]
-        return remote(part, part, r_send.at[i, c], r_recv.at[i, c], {"tp": near})
+        return remote(part, part, r_send.at[0], r_recv.at[i], {"tp": near})
 
     def z_copy(i, c):
         part = stream.at[t, rows(i), cols(c)]
-        return remote(part, part, z_send.at[i, c], z_recv.at[i, c], {"pp": jnp.minimum(sec + 1, last)})
+        return remote(part, part, z_send.at[0], z_recv.at[i, c], {"pp": jnp.minimum(sec + 1, last)})
 
     def ay_copy(i):
         part = attended.at[t, rows(i)]
-        return remote(part, part, ay_send.at[i], ay_recv.at[i], {"tp": far})
+        return remote(part, part, ay_send.at[0], ay_recv.at[i], {"tp": far})
 
     def ad_copy(i):
         part = attended.at[t, rows(i)]
-        return remote(part, part, ad_send.at[i], ad_recv.at[i], {"tp": near})
+        return remote(part, part, ad_send.at[0], ad_recv.at[i], {"tp": near})
 
     def ar_copy(i):
         part = attended.at[far, rows(i)]
-        return remote(part, part, ar_send.at[i], ar_recv.at[i], {"tp": near})
+        return remote(part, part, ar_send.at[0], ar_recv.at[i], {"tp": near})
 
     def h_copy(i):
         return remote(
             stream.at[t, rows(i)],
             landed.at[rows(i % per_section)],
-            h_send.at[i],
-            h_recv.at[i % per_section],
+            h_send.at[0],
+            h_recv.at[0],
             {"pp": i // per_section},
         )
 
+    early_mbs = 3 * M // 4
+    page_route = ((t, far), (t, near), (far, near))
+
     def k_copy(kind, i):
-        which, to = ((t, far), (t, near), (far, near))[kind]
+        which, to = page_route[kind]
         part = keyval.at[which, rows(i)]
-        return remote(part, part, k_send.at[kind, i], k_recv.at[kind, i], {"tp": to})
+        recv = k_recv.at[i] if kind == 0 else k_in.at[kind - 1, i // early_mbs]
+        return remote(part, part, k_send.at[kind], recv, {"tp": to})
+
+    def y_rows(i):
+        part = stream.at[t, rows(i)]
+        return remote(part, part, y_send.at[i], y_recv.at[i, 0], {"tp": far})
+
+    def d_rows(i):
+        part = stream.at[t, rows(i)]
+        return remote(part, part, d_send.at[i], d_recv.at[i], {"tp": near})
+
+    def r_rows(i):
+        part = stream.at[far, rows(i)]
+        return remote(part, part, r_send.at[0], r_recv.at[i], {"tp": near})
+
+    def all_sent(part, send, recv):
+        remote(part, part, send, recv, {"tp": near}).wait_send()
 
     def gain_copy(kind):
         return remote(gain_ref, gains.at[t], gain_send.at[kind], gain_recv.at[kind], {"tp": (near, far, cross)[kind]})
@@ -433,9 +454,8 @@
         ar_copy(i).start()
 
     def far_out(i):
-        for c in range(C):
-            y_copy(i, c).wait_send()
-            d_copy(i, c).wait_send()
+        y_rows(i).wait_send()
+        d_rows(i).wait_send()
         ar_copy(i).wait_recv()
         wide = 2 * chunk
         for n in range(C // 2):
@@ -456,14 +476,16 @@
     cache_rows = cache.shape[0]
     block = cache_rows // 4
     held = kv_width // (2 * HEAD_SIZE)
-    half = total_rows // 2
-
-    def assemble(n):
-        at = slice(n * half, (n + 1) * half)
+    def cache_store(b):
+        at = pl.ds(pl.multiple_of(b * block, block), block)
+        return pltpu.make_async_copy(cache.at[at], cache_hbm.at[at], cache_sem.at[0])
+
+    def assemble(lo, hi, final_part):
+        at = slice(lo * R, hi * R)
 
         def one_block(b, carry):
             start = pl.multiple_of(b * block, block)
-            row = lax.broadcasted_iota(jnp.int32, (block, half), 0)
+            row = lax.broadcasted_iota(jnp.int32, (block, (hi - lo) * R), 0)
             row = (row + t * cache_rows + start).astype(jnp.float32)
             total = jnp.zeros((block, 2 * HEAD_SIZE), jnp.float32)
             for s in range(4):
@@ -472,9 +494,11 @@
                     onehot = jnp.where(ids[head : head + 1, at] == row, 1.0, 0.0).astype(jnp.bfloat16)
                     pages = keyval[s, at, g * 2 * HEAD_SIZE : (g + 1) * 2 * HEAD_SIZE]
                     total = total + jnp.dot(onehot, pages, preferred_element_type=jnp.float32)
-            if n == 1:
+            if final_part:
                 total = total + cache[pl.ds(start, block), :].astype(jnp.float32)
             cache[pl.ds(start, block), :] = total.astype(jnp.bfloat16)
+            if final_part:
+                cache_store(b).start()
             return carry
 
         lax.fori_loop(0, 4, one_block, 0)
@@ -484,12 +508,10 @@
         k_copy(2, i).start()
 
     def pages_in(lo, hi):
-        def one_mb(i, carry):
-            k_copy(1, i).wait_recv()
-            k_copy(2, i).wait_recv()
-            return carry
-
-        lax.fori_loop(lo, hi, one_mb, 0)
+        for kind in (1, 2):
+            which, to = page_route[kind]
+            part = keyval.at[which, pl.ds(lo * R, (hi - lo) * R)]
+            remote(part, part, k_send.at[kind], k_in.at[kind - 1, lo // early_mbs], {"tp": to}).wait_recv()
 
     for kind in range(3):
         gain_copy(kind).start()
@@ -501,8 +523,7 @@
     wkv_copy(near).wait()
     for kind in range(3):
         gain_copy(kind).wait_recv()
-    for c in range(C):
-        d_copy(0, c).wait_recv()
+    d_rows(0).wait_recv()
     near_part(0)
     for c in range(C):
         relay(0, c)
@@ -527,8 +548,7 @@
 
     for c in range(C // 2, C):
         forward(1, c)
-    for c in range(C):
-        r_copy(0, c).wait_recv()
+    r_rows(0).wait_recv()
     attend(0)
     for s in sources:
         wo_copy(s).wait()
@@ -540,8 +560,7 @@
                 for c in chunks:
                     forward(i + 2, c)
 
-        for c in range(C):
-            d_copy(i + 1, c).wait_recv()
+        d_rows(i + 1).wait_recv()
         near_part(i + 1)
         ahead(first, 0, 1)
         ahead(sec > 0, 0)
@@ -555,8 +574,7 @@
         ahead(final, 3)
         relay_att(i)
         ahead(first, 3)
-        for c in range(C):
-            r_copy(i + 1, c).wait_recv()
+        r_rows(i + 1).wait_recv()
         attend(i + 1)
         ahead(middle, 3)
 
@@ -572,8 +590,8 @@
 
     @pl.when(sec == last)
     def _():
-        pages_in(0, M // 2)
-        assemble(0)
+        pages_in(0, early_mbs)
+        assemble(0, early_mbs, False)
 
     relay_att(M - 1)
 
@@ -596,10 +614,9 @@
 
         lax.fori_loop(0, M, send_pages, 0)
         lax.fori_loop(0, M, pass_pages, 0)
-        pages_in(0, M // 2)
-        assemble(0)
-        for n in range(per_section):
-            h_copy(n).wait_recv()
+        pages_in(0, early_mbs)
+        assemble(0, early_mbs, False)
+        remote(landed, landed, h_send.at[0], h_recv.at[0], {"pp": 0}).wait_recv()
         done = pltpu.make_async_copy(landed, hidden_hbm, out_sem.at[0])
         done.start()
         done.wait()
@@ -610,32 +627,24 @@
     def _():
         pltpu.make_async_copy(mine, hidden_hbm, out_sem.at[0]).start()
 
-    pages_in(M // 2, M)
-    assemble(1)
-    stored = pltpu.make_async_copy(cache, cache_hbm, out_sem.at[1])
-    stored.start()
-
-    def drain(i, carry):
-        for c in range(C):
-            r_copy(i, c).wait_send()
-
-            @pl.when(sec < last)
-            def _():
-                z_copy(i, c).wait_send()
-
-        ay_copy(i).wait_send()
-        ad_copy(i).wait_send()
-        ar_copy(i).wait_send()
-        for kind in range(3):
-            k_copy(kind, i).wait_send()
-
-        @pl.when((sec == last) & (i // per_section < last))
-        def _():
-            h_copy(i).wait_send()
-
-        return carry
-
-    lax.fori_loop(0, M, drain, 0)
+    pages_in(early_mbs, M)
+    assemble(early_mbs, M, True)
+
+    all_sent(stream.at[far], r_send.at[0], r_recv.at[0])
+    all_sent(attended.at[t], ay_send.at[0], ay_recv.at[0])
+    all_sent(attended.at[t], ad_send.at[0], ad_recv.at[0])
+    all_sent(attended.at[far], ar_send.at[0], ar_recv.at[0])
+    for kind in range(3):
+        all_sent(keyval.at[page_route[kind][0]], k_send.at[kind], k_recv.at[0])
+
+    @pl.when(sec < last)
+    def _():
+        all_sent(stream.at[t], z_send.at[0], z_recv.at[0, 0])
+
+    @pl.when(sec == last)
+    def _():
+        all_sent(stream.at[t, pl.ds(0, (M - per_section) * R)], h_send.at[0], h_recv.at[0])
+
     for kind in range(3):
         gain_copy(kind).wait_send()
 
@@ -643,7 +652,7 @@
     def _():
         pltpu.make_async_copy(mine, hidden_hbm, out_sem.at[0]).wait()
 
-    stored.wait()
+    pltpu.make_async_copy(cache, cache_hbm, cache_sem.at[0]).wait()
 
 
 def kernel_body(tokens, gain, q_weight, kv_weight, out_weight, page_table, segment_ids):
@@ -690,25 +699,27 @@
             dma((M,)),
             dma((3,)),
             dma((3,)),
+            dma((1,)),
             dma((M, C)),
+            dma((M,)),
             dma((M, C)),
-            dma((M, C)),
-            dma((M, C)),
-            dma((M, C)),
-            dma((M, C)),
-            dma((M, C)),
-            dma((M, C)),
-            dma((M,)),
-            dma((M,)),
-            dma((M,)),
-            dma((M,)),
-            dma((M,)),
-            dma((M,)),
-            dma((3, M)),
-            dma((3, M)),
-            dma((M,)),
-            dma((M // pp_size,)),
-            dma((2,)),
+            dma((M,)),
+            dma((M,)),
+            dma((1,)),
+            dma((M,)),
+            dma((1,)),
+            dma((M,)),
+            dma((1,)),
+            dma((M,)),
+            dma((1,)),
+            dma((M,)),
+            dma((3,)),
+            dma((M,)),
+            dma((2, 2)),
+            dma((1,)),
+            dma((1,)),
+            dma((1,)),
+            dma((1,)),
         ],
         compiler_params=pltpu.CompilerParams(
             collective_id=0, has_side_effects=True, vmem_limit_bytes=67043328

time: 182 us -> 180 us (0.989)
  no operation moved by 1% of the time
where the time goes in v4:
time: 180 us
  Pallas kernels  176 us (98%)
  local copies, waits for them, and re-layouts  3.84 us (2%)
    pallas_call x1, Pallas kernels, kernel_body(): pl.pallas_call(functools.partial(section_kernel, R, M, pp_size), out_shap...  176 us

profile of v4, /device:TPU:27, one launch (start us, length us, event | category | flops | bytes accessed | tf_op | source)
XLA Modules:
  0.0 180.2 jit_solution(11084992756697931782)
XLA Ops:
  0.6 175.8 %shard_map.86 = (bf16[128,2048]{1,0:T(8,128)(2,1)}, bf16[1024,256]{1,0:T(8,128)(2,1)}) custom-call(bf16[512,2048]{1,0:T(8,128)(2,1)} %tokens_hbm.1, bf16[1,2048]{1,0:T(2,128)(2,1)} %gain_ref.1, bf16[1,8192,1024]{2,1,0:T(8,128)(2,1)} %wq_hbm.1, bf16[1,8192,512]{2,1,0:T(8,128)(2,1)} %wkv_hbm.1, bf16[1,4096,2048]{2,1,0:T(8,128)(2,1)} %wo_hbm.1, ...), custom_call_target="tpu_custom_call" | custom-call | tf_op jit(solution)/shard_map/pallas_call | solution.py:673
  176.4 2.0 %reshape.7 = bf16[1,256,4,256]{3,2,1,0:T(4,128)(2,1)} reshape(bf16[1024,256]{1,0:T(8,128)(2,1)} %get-tuple-element.5) | data formatting | bytes 1048576 | tf_op jit(solution)/shard_map/reshape | solution.py:736
  178.4 1.9 %copy.10 = bf16[128,2048]{1,0:T(8,128)(2,1)} copy(bf16[128,2048]{1,0:T(8,128)(2,1)} %get-tuple-element.8) | data formatting | bytes 1048576
